TPU v7x, 1024 devices: a whole 8x8x8 slice. The times are simulated.
1024 devices in a mesh: morton: 64 (over x, y), group: 16 (over z, core).
Axes of the slice: x: 8, y: 8, z: 8, core: 2. Of those that a mesh axis runs over, the one named last changes fastest.
Arguments:
- state: float32 [16, 512, 5, 512], P('group', 'morton'), may hold values from -12 to 110, as said below
- patch_count: int32 [64], P('morton'), may hold values from 1 to 8, as said below
- neighbour_table: int32 [64, 8, 4], P('morton'), may hold values from -1 to 511, as said below
- send_table: int32 [64, 64, 5], P('morton'), may hold values from -1 to 31, as said below
- ghost_table: int32 [64, 8, 4], P('morton'), may hold values from -1 to 319, as said below
Outputs:
- updated: float32 [16, 512, 5, 512], P('group', 'morton')
Inputs may be any that keep to these rules, and one draw needn't show every extreme that they name: `state`: density lies in [0.5, 2] and the pressure implied by the five variables in [0.1, 0.4] in every live cell. `patch_count`: range i holds slab-order positions starting[i] to starting[i+1] - 1, where starting[i] = i * 4 + j[i] with |j[i]| <= 2 and j[0] = j[64] = 0; some range holds 8. `neighbour_table`: global slot = range * 8 + local slot; slab positions form rows of 4; faces 0 and 1 meet positions -4 and +4, faces 2 and 3 the neighbours in the row; empty slots and domain walls give -1. `send_table`: entry [i, j, t] is -1 or local slot * 4 + face of a patch of range i whose face goes to slot t of the message from i to j; messages of some pair use all 5 slots. `ghost_table`: -1 for faces whose neighbour is held by the same range or absent; else i * 5 + t for the face sent by range i in slot t, and i lies within 2 of the receiving range.
All inputs are finite; a program needn't handle non-finite values.
Results may differ from a plain program's by a relative error of at most 0.00002.
Values sent between devices are 32-bit elements; how exact they have to be, the bound alone decides.
A program may use at most 32 MiB of HBM per device.

v0:
```python
import jax
import jax.numpy as jnp
from jax import lax
from jax.sharding import Mesh
from jax.sharding import PartitionSpec as P

EDGE = 8
VARS = 5
MORTON = ("morton_0", "morton_1")
MORTON_GROUP = ("morton_0", "morton_1", "group_0", "group_1")
GROUP = ("group_0", "group_1")


GAMMA = 1.4
COURANT = 0.8


def over_axes(shard, axes):
    for axis in axes:
        shard = lax.pmax(shard, axis)
    return shard


def shifted(value, axis, steps):
    count = lax.axis_size(axis)
    leading, last = (max(0, -steps), min(count, count - steps))
    return lax.ppermute(value, axis, [(source, source + steps) for source in range(leading, last)])


def padded(shard, sides, width):
    for axis, dim in sides:
        peers, length = (lax.axis_size(axis), shard.shape[dim])
        up = [(i, (i + 1) % peers) for i in range(peers - 1)]
        down = [(j, i) for i, j in up]
        last = lax.slice_in_dim(shard, length - width, length, axis=dim)
        leading = lax.slice_in_dim(shard, 0, width, axis=dim)
        before = lax.ppermute(last, axis, up)
        after = lax.ppermute(leading, axis, down)
        shard = jnp.concatenate([before, shard, after], axis=dim)
    return shard


def face_layer(blocks, direction):
    if direction == 0:
        return blocks[..., 0, :, :]
    if direction == 1:
        return blocks[..., -1, :, :]
    if direction == 2:
        return blocks[..., :, 0, :]
    if direction == 3:
        return blocks[..., :, -1, :]
    if direction == 4:
        return blocks[..., :, :, 0]
    return blocks[..., :, :, -1]


def primitives(cells_flat):
    density = cells_flat[..., 0, :]
    momenta = cells_flat[..., 1:4, :]
    energy = cells_flat[..., 4, :]
    velocity = momenta / density[..., None, :]
    pressure = (GAMMA - 1.0) * (energy - 0.5 * jnp.sum(momenta * velocity, axis=-2))
    sound = jnp.sqrt(GAMMA * pressure / density)
    return (density, momenta, energy, velocity, pressure, sound)


def wave_bound(cells_flat):
    density, momenta, energy, velocity, pressure, sound = primitives(cells_flat)
    return jnp.sum(jnp.abs(velocity), axis=-2) + 3.0 * sound


def euler_flux(cells_flat, normal_axis):
    density, momenta, energy, velocity, pressure, sound = primitives(cells_flat)
    normal = velocity[..., normal_axis, :]
    parts = [momenta[..., normal_axis, :]]
    for compon in range(3):
        term = momenta[..., compon, :] * normal
        if compon == normal_axis:
            term = term + pressure
        parts.append(term)
    parts.append((energy + pressure) * normal)
    return (jnp.stack(parts, axis=-2), jnp.abs(normal) + sound)


def rusanov(left, right, normal_axis):
    flux_left, speed_left = euler_flux(left, normal_axis)
    flux_right, speed_right = euler_flux(right, normal_axis)
    speed = jnp.maximum(speed_left, speed_right)
    return 0.5 * (flux_left + flux_right) - 0.5 * speed[..., None, :] * (right - left)


def spread_face(face, normal_axis):
    if normal_axis == 0:
        widened = face[..., None, :, :]
    elif normal_axis == 1:
        widened = face[..., :, None, :]
    else:
        widened = face[..., :, :, None]
    full_shape = face.shape[:-2] + (EDGE, EDGE, EDGE)
    return jnp.broadcast_to(widened, full_shape).reshape(face.shape[:-2] + (EDGE * EDGE * EDGE,))


def divergence_flat(cells_flat, ghosts):
    cell_ids = jnp.arange(EDGE * EDGE * EDGE, dtype=jnp.int32)
    total = None
    for normal_axis in range(3):
        stride = EDGE ** (2 - normal_axis)
        position = cell_ids // stride % EDGE
        lower_full = spread_face(ghosts[2 * normal_axis], normal_axis)
        upper_full = spread_face(ghosts[2 * normal_axis + 1], normal_axis)
        left = jnp.where(position == 0, lower_full, jnp.roll(cells_flat, stride, axis=-1))
        right = jnp.where(position == EDGE - 1, upper_full, jnp.roll(cells_flat, -stride, axis=-1))
        term = rusanov(cells_flat, right, normal_axis) - rusanov(left, cells_flat, normal_axis)
        total = term if total is None else total + term
    return total


def per_device(state, patch_count, neighbour_table, send_table, ghost_table):
    slots = state.shape[1]
    message = send_table.shape[2]
    ranges = lax.axis_size(MORTON)
    myself = lax.axis_index(MORTON)
    cells_flat = state[0]
    blocks = cells_flat.reshape(slots, VARS, EDGE, EDGE, EDGE)
    valid = jnp.arange(slots, dtype=jnp.int32) < patch_count[0]
    local_top = jnp.max(jnp.where(valid[:, None], wave_bound(cells_flat), jnp.float32(0.0)))
    top_speed = over_axes(local_top, MORTON_GROUP)
    step_size = COURANT / top_speed
    layers = jnp.stack([face_layer(blocks, direction) for direction in range(4)], axis=1)
    width = VARS * EDGE * EDGE
    own_faces = layers.reshape(slots * 4, width)

    def gather_faces(table_entries):
        picked = jnp.take(own_faces, jnp.maximum(table_entries, 0), axis=0)
        return jnp.where((table_entries >= 0)[..., None], picked, jnp.float32(0.0))

    def outgoing(offset):
        wanted = jnp.clip(myself + offset, 0, ranges - 1)
        target_entries = lax.dynamic_index_in_dim(send_table[0], wanted, 0, keepdims=False)
        return gather_faces(target_entries)

    ghost_index = ghost_table[0].reshape(slots * 4)
    stacked = [jnp.zeros((message, width), jnp.float32) for number in range(5)]
    for sign in (-1, 1):
        pair = jnp.stack([outgoing(sign), outgoing(2 * sign)])
        arrived = shifted(pair, MORTON, sign)
        stacked[2 - sign] = arrived[0]
        onward = shifted(arrived[1], MORTON, sign)
        stacked[2 - 2 * sign] = onward
    received = jnp.stack(stacked).reshape(-1, width)
    lookup = jnp.where(
        ghost_index >= 0,
        (ghost_index // message - myself + 2) * message + ghost_index % message,
        -1,
    )
    remote_faces = jnp.take(received, jnp.clip(lookup, 0, 5 * message - 1), axis=0)
    neighbours = neighbour_table[0].reshape(slots * 4)
    owners = neighbours // slots
    is_local = (neighbours >= 0) & (owners == myself)
    positions = jnp.arange(slots * 4, dtype=jnp.int32)
    directions = positions % 4
    opposite = directions + 1 - 2 * (directions % 2)
    local_index = jnp.where(is_local, neighbours % slots * 4 + opposite, positions)
    local_faces = jnp.take(own_faces, local_index, axis=0)
    ghost_faces = jnp.where((ghost_index >= 0)[:, None], remote_faces, local_faces)
    lateral = ghost_faces.reshape(slots, 4, VARS, EDGE, EDGE)
    vertical = jnp.stack([face_layer(blocks, 4), face_layer(blocks, 5)])
    extended = padded(vertical, ((GROUP, 0),), 1)
    slab_index = lax.axis_index(GROUP)
    lower = jnp.where(slab_index == 0, vertical[0], extended[0])
    upper = jnp.where(slab_index == lax.axis_size(GROUP) - 1, vertical[1], extended[3])
    ghosts = [lateral[:, direction] for direction in range(4)] + [lower, upper]
    change = divergence_flat(cells_flat, ghosts)
    result = jnp.where(valid[:, None, None], cells_flat - step_size * change, jnp.float32(0.0))
    return result.reshape(1, slots, VARS, EDGE * EDGE * EDGE)


def solution(mesh):
    torus = Mesh(mesh.devices.reshape(8, 8, 8, 2), ("morton_0", "morton_1", "group_0", "group_1"))
    return jax.shard_map(
        per_device,
        mesh=torus,
        in_specs=(
            P(GROUP, MORTON, None, None),
            P(MORTON),
            P(MORTON, None, None),
            P(MORTON, None, None),
            P(MORTON, None, None),
        ),
        out_specs=P(GROUP, MORTON, None, None),
        check_vma=False,
    )
```

profile of v0, /device:TPU:2, one launch (start us, length us, event | category | flops | bytes accessed | tf_op | source)
XLA Modules:
  0.0 168.1 jit_solution(4559227992206799856)
XLA Ops:
  0.0 1.3 maximum_reduce_fusion.1
  1.3 1.4 compare_reduce_fusion.1
  2.7 1.6 reshape_squeeze.9
  6.9 3.6 %collective-permute-start = (f32[2,5,320]{2,1,0:T(8,128)}, f32[2,5,320]{2,1,0:T(8,128)}, u32[]{:S(2)}, u32[]{:S(2)}) collective-permute-start(f32[2,5,320]{2,1,0:T(8,128)} %pad_maximum_fusion.1), channel_id=1, source_target_pairs={{0,16},{16,32},{32,48},{48,64},{64,80},{80,96},{96,112},{112,128},... | collective-permute-start | bytes 38408 | tf_op jit(solution)/shard_map/ppermute | solution.py:27
  12.4 4.5 %collective-permute-start.2 = (f32[2,5,320]{2,1,0:T(8,128)}, f32[2,5,320]{2,1,0:T(8,128)}, u32[]{:S(2)}, u32[]{:S(2)}) collective-permute-start(f32[2,5,320]{2,1,0:T(8,128)} %pad_maximum_fusion.2), channel_id=1, source_target_pairs={{16,0},{32,16},{48,32},{64,48},{80,64},{96,80},{112,96},{128,112},... | collective-permute-start | bytes 38408 | tf_op jit(solution)/shard_map/ppermute | solution.py:27
  16.9 1.5 fusion.89
  18.4 3.9 %copy.87 = f32[8,5,8,8,1]{3,2,1,0,4:T(8,128)} copy(f32[8,5,8,8,1]{4,3,2,0,1:T(8,128)} %get-tuple-element.38) | data formatting | bytes 20480 | tf_op jit(solution)/shard_map/slice | solution.py:53
  23.6 2.6 %copy.92 = f32[8,5,8,8,1]{3,2,1,0,4:T(8,128)} copy(f32[8,5,8,8,1]{4,3,2,0,1:T(8,128)S(1)} %get-tuple-element.37) | data formatting | bytes 20480 | tf_op jit(solution)/shard_map/slice | solution.py:54
  26.2 3.0 %collective-permute-start.5 = (f32[1,8,5,8,8]{4,3,2,1,0:T(8,128)}, f32[1,8,5,8,8]{4,3,2,1,0:T(8,128)S(1)}, u32[]{:S(2)}, u32[]{:S(2)}) collective-permute-start(f32[1,8,5,8,8]{4,3,2,1,0:T(8,128)} %bitcast.97), channel_id=1, source_target_pairs={{0,1},{1,2},{2,3},{3,4},{4,5},{5,6},{6,7},{7,8},{8,9},{9,10},{10,1... | collective-permute-start | bytes 30728 | tf_op jit(solution)/shard_map/ppermute | solution.py:37
  37.8 23.0 %pmax.28 = f32[]{:T(128)} all-reduce(f32[]{:T(128)} %fusion.44), channel_id=1, replica_groups=mesh['morton_0'=8,'morton_1'=8,'group_0'=8,'group_1'=2] {'morton_0'}, use_global_device_ids=true, to_apply=%region_3.4 | all-reduce | flops 1 | bytes 8 | tf_op jit(solution)/shard_map/pmax | solution.py:20
  61.4 17.4 %pmax.29 = f32[]{:T(128)} all-reduce(f32[]{:T(128)} %pmax.28), channel_id=1, replica_groups=mesh['morton_0'=8,'morton_1'=8,'group_0'=8,'group_1'=2] {'morton_1'}, use_global_device_ids=true, to_apply=%region_4.5 | all-reduce | flops 1 | bytes 8 | tf_op jit(solution)/shard_map/pmax | solution.py:20
  78.8 23.4 %pmax.30 = f32[]{:T(128)} all-reduce(f32[]{:T(128)} %pmax.29), channel_id=1, replica_groups=mesh['morton_0'=8,'morton_1'=8,'group_0'=8,'group_1'=2] {'group_0'}, use_global_device_ids=true, to_apply=%region_5.6 | all-reduce | flops 1 | bytes 8 | tf_op jit(solution)/shard_map/pmax | solution.py:20
  102.2 2.9 %pmax.31 = f32[]{:T(128)} all-reduce(f32[]{:T(128)} %pmax.30), channel_id=1, replica_groups=mesh['morton_0'=8,'morton_1'=8,'group_0'=8,'group_1'=2] {'group_1'}, use_global_device_ids=true, to_apply=%region_6.7 | all-reduce | flops 1 | bytes 8 | tf_op jit(solution)/shard_map/pmax | solution.py:20
  109.2 2.8 %copy.93 = f32[8,5,8,8,1]{4,3,2,0,1:T(8,128)S(1)} copy(f32[8,5,8,8,1]{3,2,1,0,4:T(8,128)} %bitcast.407) | data formatting | bytes 20480 | tf_op jit(solution)/shard_map/squeeze | solution.py:170
  112.0 3.9 %copy.88 = f32[8,5,8,8,1]{4,3,2,0,1:T(8,128)} copy(f32[8,5,8,8,1]{3,2,1,0,4:T(8,128)} %bitcast.84) | data formatting | bytes 20480 | tf_op jit(solution)/shard_map/squeeze | solution.py:171
  115.9 3.4 %broadcast_select_fusion = (f32[8,5,8,8,1]{4,3,2,0,1:T(8,128)}, f32[8,5,8,8,1]{4,3,2,0,1:T(8,128)}) fusion(f32[8,5,8,8,1]{4,3,2,0,1:T(8,128)S(1)} %copy.93, pred[]{:T(512)S(6)} %eq.70, f32[8,5,8,8,8]{4,3,2,0,1:T(8,128)S(1)} %reshape_squeeze.9, f32[8,5,8,8,1]{4,3,2,0,1:T(8,128)} %copy.88, pred[]{:T(512)S(6)} %eq.68), kind=kLoop, calls=%fused_computation.8 | loop fusion | flops 5120 | bytes 61442 | tf_op jit(solution)/shard_map/jit(_where)/select_n | solution.py:170
  119.3 4.0 %copy.99 = f32[8,5,8,8,1]{3,2,0,1,4:T(8,128)} copy(f32[8,5,8,8,1]{4,3,2,0,1:T(8,128)} %get-tuple-element.35) | data formatting | bytes 20480 | tf_op jit(solution)/shard_map/broadcast_in_dim | solution.py:100
  123.3 1.9 %copy.98 = f32[8,5,8,8,1]{3,2,0,1,4:T(8,128)S(1)} copy(f32[8,5,8,8,1]{4,3,2,0,1:T(8,128)S(1)} %copy-done.1) | data formatting | bytes 20480 | tf_op jit(solution)/shard_map/broadcast_in_dim | solution.py:100
  126.9 1.3 broadcast_in_dim.213
  136.3 2.8 %collective-permute-start.1 = (f32[5,320]{1,0:T(8,128)S(1)}, f32[5,320]{1,0:T(8,128)S(1)}, u32[]{:S(2)}, u32[]{:S(2)}) collective-permute-start(f32[5,320]{1,0:T(8,128)S(1)} %slice_bitcast_fusion.14), channel_id=1, source_target_pairs={{0,16},{16,32},{32,48},{48,64},{64,80},{80,96},{96,112},{112,128},... | collective-permute-start | bytes 19208 | tf_op jit(solution)/shard_map/ppermute | solution.py:27
  139.7 4.3 %collective-permute-done.1 = f32[5,320]{1,0:T(8,128)S(1)} collective-permute-done((f32[5,320]{1,0:T(8,128)S(1)}, f32[5,320]{1,0:T(8,128)S(1)}, u32[]{:S(2)}, u32[]{:S(2)}) %collective-permute-start.1) | collective-permute-done | bytes 6432 | tf_op jit(solution)/shard_map/ppermute | solution.py:27
  146.5 1.3 slice_bitcast_fusion.13
  147.9 2.9 %collective-permute-start.3 = (f32[5,320]{1,0:T(8,128)}, f32[5,320]{1,0:T(8,128)}, u32[]{:S(2)}, u32[]{:S(2)}) collective-permute-start(f32[5,320]{1,0:T(8,128)} %get-tuple-element.87), channel_id=1, source_target_pairs={{16,0},{32,16},{48,32},{64,48},{80,64},{96,80},{112,96},{128,112},... | collective-permute-start | bytes 19208 | tf_op jit(solution)/shard_map/ppermute | solution.py:27
  166.2 1.8 %fusion.8 = f32[1,8,5,512]{3,1,2,0:T(8,128)} fusion(f32[1,8,5,512]{3,1,2,0:T(8,128)S(1)} %copy-done, f32[1,8,5,512]{3,1,2,0:T(8,128)S(1)} %reshape.1552, f32[1,8,5,64]{3,1,2,0:T(8,128)S(1)} %copy-done.26, f32[1,8,5,448]{3,1,2,0:T(8,128)S(1)} %copy-done.8, f32[1,8,5,512]{3,1,2,0:T(8,128)S(1)} %reshape.1554, f32[1,8,5,448]{3,1,2,0:T(8,128)S(1)} %copy-done.9, ...), kind=kLoop, calls=%fused_computation.76 | loop fusion | flops 1024000 | bytes 1985548 | tf_op jit(solution)/shard_map/jit(_where)/select_n | solution.py:174
  (245 shorter events, 44.9 us)
Async XLA Ops:
  6.9 128.7 %collective-permute-start = (f32[2,5,320]{2,1,0:T(8,128)}, f32[2,5,320]{2,1,0:T(8,128)}, u32[]{:S(2)}, u32[]{:S(2)}) collective-permute-start(f32[2,5,320]{2,1,0:T(8,128)} %pad_maximum_fusion.1), channel_id=1, source_target_pairs={{0,16},{16,32},{32,48},{48,64},{64,80},{80,96},{96,112},{112,128},... | collective-permute-start | bytes 38408 | tf_op jit(solution)/shard_map/ppermute | solution.py:27
  12.4 134.1 %collective-permute-start.2 = (f32[2,5,320]{2,1,0:T(8,128)}, f32[2,5,320]{2,1,0:T(8,128)}, u32[]{:S(2)}, u32[]{:S(2)}) collective-permute-start(f32[2,5,320]{2,1,0:T(8,128)} %pad_maximum_fusion.2), channel_id=1, source_target_pairs={{16,0},{32,16},{48,32},{64,48},{80,64},{96,80},{112,96},{128,112},... | collective-permute-start | bytes 38408 | tf_op jit(solution)/shard_map/ppermute | solution.py:27
  18.4 10.9 %copy-start.34 = (s32[1,8,4]{1,2,0:T(4,128)S(1)}, s32[1,8,4]{1,2,0:T(4,128)}, u32[]{:S(2)}) copy-start(s32[1,8,4]{1,2,0:T(4,128)} %param.9) | copy-start | bytes 388
  18.4 11.0 %copy-start.35 = (s32[1,8,4]{1,2,0:T(4,128)S(1)}, s32[1,8,4]{1,2,0:T(4,128)}, u32[]{:S(2)}) copy-start(s32[1,8,4]{1,2,0:T(4,128)} %param.11) | copy-start | bytes 388
  18.4 11.0 %copy-start = (f32[1,8,5,512]{3,1,2,0:T(8,128)S(1)}, f32[1,8,5,512]{3,1,2,0:T(8,128)}, u32[]{:S(2)}) copy-start(f32[1,8,5,512]{3,1,2,0:T(8,128)} %param.7) | copy-start | bytes 245764
  22.4 89.7 %collective-permute-start.4 = (f32[1,8,5,8,8]{4,3,2,1,0:T(8,128)}, f32[1,8,5,8,8]{4,3,2,1,0:T(8,128)}, u32[]{:S(2)}, u32[]{:S(2)}) collective-permute-start(f32[1,8,5,8,8]{4,3,2,1,0:T(8,128)} %bitcast.83), channel_id=1, source_target_pairs={{1,0},{2,1},{3,2},{4,3},{5,4},{6,5},{7,6},{8,7},{9,8},{10,9},{11,1... | collective-permute-start | bytes 30728 | tf_op jit(solution)/shard_map/ppermute | solution.py:38
  26.2 82.2 %collective-permute-start.5 = (f32[1,8,5,8,8]{4,3,2,1,0:T(8,128)}, f32[1,8,5,8,8]{4,3,2,1,0:T(8,128)S(1)}, u32[]{:S(2)}, u32[]{:S(2)}) collective-permute-start(f32[1,8,5,8,8]{4,3,2,1,0:T(8,128)} %bitcast.97), channel_id=1, source_target_pairs={{0,1},{1,2},{2,3},{3,4},{4,5},{5,6},{6,7},{7,8},{8,9},{9,10},{10,1... | collective-permute-start | bytes 30728 | tf_op jit(solution)/shard_map/ppermute | solution.py:37
  35.1 71.3 %copy-start.36 = (pred[8]{0:T(512)(128)(4,1)}, pred[8]{0:T(512)(128)(4,1)S(1)}, u32[]{:S(2)}) copy-start(pred[8]{0:T(512)(128)(4,1)S(1)} %iota_compare_fusion) | copy-start | bytes 28
  36.6 71.9 %copy-start.19 = (f32[8,512]{1,0:T(8,128)}, f32[8,512]{1,0:T(8,128)S(1)}, u32[]{:S(2)}) copy-start(f32[8,512]{1,0:T(8,128)S(1)} %get-tuple-element.7) | copy-start | bytes 49156
  78.8 50.8 %copy-start.42 = (pred[512]{0:T(512)(128)(4,1)}, pred[512]{0:T(512)(128)(4,1)S(1)}, u32[]{:S(2)}) copy-start(pred[512]{0:T(512)(128)(4,1)S(1)} %fusion.52) | copy-start | bytes 1540
  102.2 27.3 %copy-start.44 = (pred[512]{0:T(512)(128)(4,1)}, pred[512]{0:T(512)(128)(4,1)S(1)}, u32[]{:S(2)}) copy-start(pred[512]{0:T(512)(128)(4,1)S(1)} %fusion.51) | copy-start | bytes 1540
  119.3 4.0 %copy-start.1 = (f32[8,5,8,8,1]{4,3,2,0,1:T(8,128)S(1)}, f32[8,5,8,8,1]{4,3,2,0,1:T(8,128)}, u32[]{:S(2)}) copy-start(f32[8,5,8,8,1]{4,3,2,0,1:T(8,128)} %get-tuple-element.36) | copy-start | bytes 30724
  126.9 2.6 %copy-start.32 = (f32[8,5,1]{2,0,1:T(8,128)S(1)}, f32[8,5,1]{2,0,1:T(8,128)}, u32[]{:S(2)}) copy-start(f32[8,5,1]{2,0,1:T(8,128)} %get-tuple-element.78) | copy-start | bytes 484
  126.9 2.6 %copy-start.33 = (f32[8,5,1]{2,0,1:T(8,128)S(1)}, f32[8,5,1]{2,0,1:T(8,128)}, u32[]{:S(2)}) copy-start(f32[8,5,1]{2,0,1:T(8,128)} %get-tuple-element.81) | copy-start | bytes 484
  130.7 20.1 %copy-start.2 = (f32[8,5,512]{2,0,1:T(8,128)}, f32[8,5,512]{2,0,1:T(8,128)S(1)}, u32[]{:S(2)}) copy-start(f32[8,5,512]{2,0,1:T(8,128)S(1)} %get-tuple-element.101) | copy-start | bytes 245764
  131.9 18.8 %copy-start.3 = (f32[8,3,512]{2,0,1:T(8,128)}, f32[8,3,512]{2,0,1:T(8,128)S(1)}, u32[]{:S(2)}) copy-start(f32[8,3,512]{2,0,1:T(8,128)S(1)} %get-tuple-element.31) | copy-start | bytes 147460
  132.0 18.8 %copy-start.16 = (f32[8,512]{1,0:T(8,128)}, f32[8,512]{1,0:T(8,128)S(1)}, u32[]{:S(2)}) copy-start(f32[8,512]{1,0:T(8,128)S(1)} %get-tuple-element.30) | copy-start | bytes 49156
  136.3 7.7 %collective-permute-start.1 = (f32[5,320]{1,0:T(8,128)S(1)}, f32[5,320]{1,0:T(8,128)S(1)}, u32[]{:S(2)}, u32[]{:S(2)}) collective-permute-start(f32[5,320]{1,0:T(8,128)S(1)} %slice_bitcast_fusion.14), channel_id=1, source_target_pairs={{0,16},{16,32},{32,48},{48,64},{64,80},{80,96},{96,112},{112,128},... | collective-permute-start | bytes 19208 | tf_op jit(solution)/shard_map/ppermute | solution.py:27
  147.9 6.1 %collective-permute-start.3 = (f32[5,320]{1,0:T(8,128)}, f32[5,320]{1,0:T(8,128)}, u32[]{:S(2)}, u32[]{:S(2)}) collective-permute-start(f32[5,320]{1,0:T(8,128)} %get-tuple-element.87), channel_id=1, source_target_pairs={{16,0},{32,16},{48,32},{64,48},{80,64},{96,80},{112,96},{128,112},... | collective-permute-start | bytes 19208 | tf_op jit(solution)/shard_map/ppermute | solution.py:27
  163.0 1.5 copy-start.20
  164.6 1.5 copy-start.4
  164.6 1.5 copy-start.5
  164.6 1.5 copy-start.6
  164.6 1.5 copy-start.7
  (28 other events, 37.8 us)
where the time goes:
time: 169 us; the launch traced here: 168 us
  blocking collectives  66.7 us (39%)
  local copies, waits for them, and re-layouts  56.2 us (33%)
  other arithmetic  20.3 us (12%)
  starting transfers between devices  18 us (11%)
  waiting for transfers between devices  4.31 us (3%)
  between operations  2.48 us (1%)
    pmax x4, blocking collectives, over_axes(): shard = lax.pmax(shard, axis)  66.7 us
    ppermute x4, starting transfers between devices, shifted(): lax.ppermute(value, axis, [(source, source + steps) for source in range(l...  13.7 us
    reshape x12, local copies, waits for them, and re-layouts, spread_face(): jnp.broadcast_to(widened, full_shape)  10.5 us
    broadcast_in_dim x13, local copies, waits for them, and re-layouts, spread_face(): jnp.broadcast_to(widened, full_shape)  8.27 us
    unnamed x103, local copies, waits for them, and re-layouts  5.27 us
    ppermute x4, waiting for transfers between devices, shifted(): lax.ppermute(value, axis, [(source, source + steps) for source in range(l...  4.31 us
    slice x2, local copies, waits for them, and re-layouts, face_layer(): return blocks[..., :, :, -1]  4.13 us
    slice x1, local copies, waits for them, and re-layouts, face_layer(): return blocks[..., :, :, 0]  3.94 us
  transfers between devices with their start and end apart: 6, of which 1 were waited for; matrix products, arithmetic and copies ran while one was open for 32% of the time, Pallas kernels for 0%

commit v1 on v0

v1 whole, which is shorter than its diff:
```python
import functools

import jax
import jax.numpy as jnp
from jax import lax
from jax.experimental import pallas as pl
from jax.experimental.pallas import tpu as pltpu
from jax.sharding import Mesh
from jax.sharding import PartitionSpec as P

EDGE = 8
VARS = 5
CELLS = EDGE * EDGE * EDGE
FACE = EDGE * EDGE
SLOTS = 8
MSG = 5
LANES = 128
WIDE = 384
GAMMA = 1.4
COURANT = 0.8
AXES = ("morton_0", "morton_1", "group_0", "group_1")
MORTON = ("morton_0", "morton_1")
GROUP = ("group_0", "group_1")
OFFSETS = (-2, -1, 1, 2)
HUB = 1


def primitives(cells):
    density, mx, my, mz, energy = cells
    inverse = 1.0 / density
    velocity = (mx * inverse, my * inverse, mz * inverse)
    kinetic = mx * velocity[0] + my * velocity[1] + mz * velocity[2]
    pressure = (GAMMA - 1.0) * (energy - 0.5 * kinetic)
    sound = jnp.sqrt(GAMMA * pressure * inverse)
    return velocity, pressure, sound


def axis_flux(cells, prims, axis):
    velocity, pressure, sound = prims
    normal = velocity[axis]
    parts = [cells[1 + axis]]
    for comp in range(3):
        term = cells[1 + comp] * normal
        parts.append(term + pressure if comp == axis else term)
    parts.append((cells[4] + pressure) * normal)
    return parts, jnp.abs(normal) + sound


def lane(shape):
    return lax.broadcasted_iota(jnp.int32, shape, 1)


def pick_lanes(tile, index):
    return jnp.take_along_axis(tile, index, axis=1, mode="promise_in_bounds")


def tiles_of(wide):
    return [wide[:, q * LANES:(q + 1) * LANES] for q in range(wide.shape[1] // LANES)]


def pack_face(cells, face):
    axis, far = face // 2, face % 2
    if axis == 0:
        parts = [v[:, CELLS - FACE:] if far else v[:, :FACE] for v in cells]
        parts.append(jnp.zeros((SLOTS, FACE), jnp.float32))
        return jnp.concatenate(parts, axis=1)
    at = lane((SLOTS, LANES))
    place = at & (FACE - 1)
    if axis == 1:
        source = ((place >> 3) & 1) * FACE + far * (FACE - EDGE) + (place & 7)
    else:
        source = (place & 15) * EDGE + far * (EDGE - 1)
    packed = []
    for v in cells:
        tiles = tiles_of(v)
        out = pick_lanes(tiles[0], source)
        for q in range(1, 4):
            out = jnp.where((place >> 4) == q, pick_lanes(tiles[q], source), out)
        packed.append(out)
    packed.append(jnp.zeros((SLOTS, LANES), jnp.float32))
    pairs = [jnp.where(at < FACE, packed[2 * j], packed[2 * j + 1]) for j in range(3)]
    return jnp.concatenate(pairs, axis=1)


def spread_face(packed, var, axis):
    tile = tiles_of(packed)[var // 2]
    base = (var % 2) * FACE
    at = lane((SLOTS, LANES))
    if axis == 0:
        one = pick_lanes(tile, base + (at & (FACE - 1)))
        return jnp.concatenate([one] * 4, axis=1)
    out = []
    for q in range(4):
        if axis == 1:
            index = base + q * 16 + (at >> 6) * EDGE + (at & 7)
        else:
            index = base + q * 16 + (at >> 3)
        out.append(pick_lanes(tile, index))
    return jnp.concatenate(out, axis=1)


def diagonal(row):
    shape = (SLOTS, SLOTS)
    keep = lax.broadcasted_iota(jnp.int32, shape, 0) == lane(shape)
    return jnp.sum(jnp.where(keep, jnp.broadcast_to(row, shape), 0.0), axis=1, keepdims=True)


def one_hot(column, width):
    places = lane((column.shape[0], width)).astype(jnp.float32)
    return (column == places).astype(jnp.float32)


def select_rows(hot, table):
    return jnp.dot(hot, table, precision=lax.Precision.HIGHEST, preferred_element_type=jnp.float32)


def kernel(
    sizes,
    state, count, neighbour, send, ghost,
    kept_out, change_out, top_out,
    cells_ref, count_ref, neighbour_ref, send_ref, ghost_ref,
    vertical_out, vertical_in, lateral_out, lateral_in,
    value, from_z, from_x, from_y,
    load_sem, count_sem, table_sem, up_sem, down_sem, vin_sem, lsend_sem, lin_sem, max_send, max_recv,
):
    nx, ny, nz, nc = sizes
    x, y, z, c = [lax.axis_index(a) for a in AXES]
    rank = x * ny + y
    ranks = nx * ny

    def device(px, py, pz, pc):
        return {"morton_0": px, "morton_1": py, "group_0": pz, "group_1": pc}

    def at_rank(offset):
        j = lax.rem(rank + (offset + ranks), ranks)
        return device(lax.div(j, ny), lax.rem(j, ny), z, c)

    other = 1 - c
    below = device(x, y, lax.rem(z + (nz - 1) + c, nz), other)
    above = device(x, y, lax.rem(z + c, nz), other)

    loads = [
        pltpu.make_async_copy(state.at[0], cells_ref, load_sem),
        pltpu.make_async_copy(count, count_ref, count_sem),
        pltpu.make_async_copy(neighbour.at[0], neighbour_ref, table_sem.at[0]),
        pltpu.make_async_copy(send, send_ref, table_sem.at[1]),
        pltpu.make_async_copy(ghost.at[0], ghost_ref, table_sem.at[2]),
    ]
    for load in loads:
        load.start()

    barrier = pltpu.get_barrier_semaphore()

    def greet(target):
        pl.semaphore_signal(barrier, inc=1, device_id=target, device_id_type=pl.DeviceIdType.MESH)

    def on(axis_size, here, step):
        return lax.rem(here + step, axis_size)

    hub_partners = (nz - 1) + (nx - 1) + (ny - 1) * 2 + 1
    for target in [below, above] + [at_rank(o) for o in OFFSETS]:
        greet(target)

    @pl.when(c == HUB)
    def _():
        for step in range(1, nz):
            greet(device(x, y, on(nz, z, step), HUB))
        for step in range(nz):
            greet(device(x, y, on(nz, z, step), 1 - HUB))
        for step in range(1, nx):
            greet(device(on(nx, x, step), y, z, HUB))
        for step in range(1, ny):
            greet(device(x, on(ny, y, step), z, HUB))

    @pl.when(c != HUB)
    def _():
        for step in range(ny):
            greet(device(x, on(ny, y, step), z, HUB))

    loads[1].wait()
    loads[0].wait()
    live = lax.broadcasted_iota(jnp.int32, (SLOTS, CELLS), 0) < count_ref[0]
    cells = [cells_ref[v] for v in range(VARS)]
    prims = primitives(cells)
    velocity, pressure, sound = prims
    speed = jnp.abs(velocity[0]) + jnp.abs(velocity[1]) + jnp.abs(velocity[2]) + 3.0 * sound
    speed = jnp.where(live, speed, 0.0)
    top = jnp.max(functools.reduce(jnp.maximum, tiles_of(speed)), axis=0, keepdims=True)
    value[0] = top

    @pl.when(c == HUB)
    def _():
        from_z[z * 2 + HUB] = top
        pl.semaphore_wait(barrier, hub_partners + 2 * 3)

    @pl.when(c != HUB)
    def _():
        pl.semaphore_wait(barrier, nz + 2 * 3)

    def push(source, target_ref, target, phase):
        copy = pltpu.make_async_remote_copy(
            src_ref=source, dst_ref=target_ref, send_sem=max_send.at[phase], recv_sem=max_recv.at[phase],
            device_id=target, device_id_type=pl.DeviceIdType.MESH)
        copy.start()

    def settle(ref, number, sem):
        pltpu.make_async_copy(ref.at[pl.ds(0, number)], ref.at[pl.ds(0, number)], sem).wait()

    def highest(ref, number):
        return functools.reduce(jnp.maximum, [ref[i] for i in range(number)])

    for step in range(1, nz):
        push(value.at[0], from_z.at[z * 2 + c], device(x, y, on(nz, z, step), HUB), 0)

    @pl.when(c != HUB)
    def _():
        push(value.at[0], from_z.at[z * 2 + c], device(x, y, z, HUB), 0)

    vertical_out[0] = pack_face(cells, 4)
    vertical_out[1] = pack_face(cells, 5)
    go_down = pltpu.make_async_remote_copy(
        src_ref=vertical_out.at[0], dst_ref=vertical_in.at[1], send_sem=down_sem, recv_sem=vin_sem.at[1],
        device_id=below, device_id_type=pl.DeviceIdType.MESH)
    go_up = pltpu.make_async_remote_copy(
        src_ref=vertical_out.at[1], dst_ref=vertical_in.at[0], send_sem=up_sem, recv_sem=vin_sem.at[0],
        device_id=above, device_id_type=pl.DeviceIdType.MESH)
    go_down.start()
    go_up.start()

    own = [pack_face(cells, face) for face in range(4)]
    own_rows = jnp.concatenate(own, axis=0)
    loads[3].wait()
    rows = jnp.concatenate([send_ref[t] for t in range(MSG)] + [jnp.full((SLOTS - MSG, ranks), -1, jnp.int32)], axis=0)
    columns = []
    for offset in OFFSETS:
        j = lax.rem(rank + (offset + ranks), ranks)
        picked = jnp.where(lane((SLOTS, ranks)) == j, rows, 0).astype(jnp.float32)
        entry = jnp.sum(picked, axis=1, keepdims=True)
        entry_int = entry.astype(jnp.int32)
        row = jnp.where(entry_int >= 0, (entry_int & 3) * SLOTS + (entry_int >> 2), -1)
        columns.append(row.astype(jnp.float32))
    hot = one_hot(jnp.concatenate(columns, axis=0), 4 * SLOTS)
    messages = select_rows(hot, own_rows)
    for d in range(4):
        lateral_out[d] = messages[d * SLOTS:(d + 1) * SLOTS]
    lateral = []
    for d, offset in enumerate(OFFSETS):
        copy = pltpu.make_async_remote_copy(
            src_ref=lateral_out.at[d], dst_ref=lateral_in.at[3 - d], send_sem=lsend_sem.at[d], recv_sem=lin_sem.at[3 - d],
            device_id=at_rank(offset), device_id_type=pl.DeviceIdType.MESH)
        copy.start()
        lateral.append(copy)

    @pl.when(c == HUB)
    def _():
        settle(from_z, 2 * nz - 1, max_recv.at[0])
        along_z = highest(from_z, 2 * nz)
        value[1] = along_z
        from_x[x] = along_z
        for step in range(1, nx):
            push(value.at[1], from_x.at[x], device(on(nx, x, step), y, z, HUB), 1)

    loads[2].wait()
    loads[4].wait()
    go_down.wait_recv()
    go_up.wait_recv()
    for d in range(4):
        pltpu.make_async_remote_copy(
            src_ref=lateral_out.at[d], dst_ref=lateral_in.at[d], send_sem=lsend_sem.at[d], recv_sem=lin_sem.at[d],
            device_id=at_rank(1), device_id_type=pl.DeviceIdType.MESH).wait_recv()
    faces = jnp.concatenate([own_rows] + [lateral_in[d] for d in range(4)], axis=0)
    near = neighbour_ref[...]
    far = ghost_ref[...]
    face_id = lax.broadcasted_iota(jnp.int32, (4, SLOTS), 0)
    slot_id = lane((4, SLOTS))
    local = (near >= 0) & ((near >> 3) == rank)
    place = jnp.where(local, (face_id ^ 1) * SLOTS + (near & 7), face_id * SLOTS + slot_id)
    relative = far - rank * MSG + 2 * MSG
    block = sum((relative >= MSG * k).astype(jnp.int32) for k in range(1, 5))
    remote = 4 * SLOTS + SLOTS * (block - (block > 2).astype(jnp.int32)) + relative - MSG * block
    place = jnp.where(far >= 0, jnp.where(block == 2, -1, remote), place).astype(jnp.float32)
    columns = [diagonal(place[k:k + 1, :]) for k in range(4)]
    hot = one_hot(jnp.concatenate(columns, axis=0), 8 * SLOTS)
    chosen = select_rows(hot, faces)
    ghosts = [chosen[k * SLOTS:(k + 1) * SLOTS] for k in range(4)]
    slab = z * nc + c
    ghosts.append(jnp.where(slab == 0, vertical_out[0], vertical_in[0]))
    ghosts.append(jnp.where(slab == nz * nc - 1, vertical_out[1], vertical_in[1]))

    total = [0.0] * VARS
    at = lane((SLOTS, CELLS))
    for axis in range(3):
        stride = EDGE ** (2 - axis)
        position = (at >> (3 * (2 - axis))) & 7
        low = [jnp.where(position == 0, spread_face(ghosts[2 * axis], v, axis), pltpu.roll(cells[v], stride, 1))
               for v in range(VARS)]
        high = [jnp.where(position == EDGE - 1, spread_face(ghosts[2 * axis + 1], v, axis),
                          pltpu.roll(cells[v], CELLS - stride, 1)) for v in range(VARS)]
        flux_low, speed_low = axis_flux(low, primitives(low), axis)
        flux_high, speed_high = axis_flux(high, primitives(high), axis)
        speed_here = jnp.abs(velocity[axis]) + sound
        lower = jnp.maximum(speed_low, speed_here)
        upper = jnp.maximum(speed_here, speed_high)
        for v in range(VARS):
            total[v] = total[v] + 0.5 * (
                (flux_high[v] - flux_low[v]) - (upper * (high[v] - cells[v]) - lower * (cells[v] - low[v])))
    for v in range(VARS):
        kept_out[v] = jnp.where(live, cells[v], 0.0)
        change_out[v] = jnp.where(live, total[v], 0.0)

    @pl.when(c == HUB)
    def _():
        settle(from_x, nx - 1, max_recv.at[1])
        plane = highest(from_x, nx)
        value[2] = plane
        from_y[y] = plane
        push(value.at[2], from_y.at[y], device(x, y, z, 1 - HUB), 2)
        for step in range(1, ny):
            push(value.at[2], from_y.at[y], device(x, on(ny, y, step), z, HUB), 2)
            push(value.at[2], from_y.at[y], device(x, on(ny, y, step), z, 1 - HUB), 2)
        settle(from_y, ny - 1, max_recv.at[2])

    @pl.when(c != HUB)
    def _():
        settle(from_y, ny, max_recv.at[2])

    over_all = jnp.max(highest(from_y, ny), axis=1, keepdims=True)
    top_out[...] = jnp.broadcast_to(COURANT / over_all, (1, LANES))

    go_down.wait_send()
    go_up.wait_send()
    for copy in lateral:
        copy.wait_send()

    @pl.when(c == HUB)
    def _():
        settle(from_z, nz - 1, max_send.at[0])
        settle(from_x, nx - 1, max_send.at[1])
        settle(from_z, 2 * ny - 1, max_send.at[2])

    @pl.when(c != HUB)
    def _():
        settle(from_z, nz, max_send.at[0])


def per_device(sizes, state, patch_count, neighbour_table, send_table, ghost_table):
    nx, ny, nz, nc = sizes
    any_space = pl.BlockSpec(memory_space=pl.ANY)
    vmem = pl.BlockSpec(memory_space=pltpu.VMEM)
    f32 = jnp.float32
    dma = pltpu.SemaphoreType.DMA
    kept, change, step = pl.pallas_call(
        functools.partial(kernel, sizes),
        out_shape=(
            jax.ShapeDtypeStruct((VARS, SLOTS, CELLS), f32),
            jax.ShapeDtypeStruct((VARS, SLOTS, CELLS), f32),
            jax.ShapeDtypeStruct((1, LANES), f32),
        ),
        in_specs=[any_space] * 5,
        out_specs=(vmem, vmem, vmem),
        scratch_shapes=[
            pltpu.VMEM((VARS, SLOTS, CELLS), f32),
            pltpu.SMEM((1,), jnp.int32),
            pltpu.VMEM((4, SLOTS), jnp.int32),
            pltpu.VMEM((MSG, 1, nx * ny), jnp.int32),
            pltpu.VMEM((4, SLOTS), jnp.int32),
            pltpu.VMEM((2, SLOTS, WIDE), f32),
            pltpu.VMEM((2, SLOTS, WIDE), f32),
            pltpu.VMEM((4, SLOTS, WIDE), f32),
            pltpu.VMEM((4, SLOTS, WIDE), f32),
            pltpu.VMEM((3, 1, LANES), f32),
            pltpu.VMEM((2 * max(nz, ny), 1, LANES), f32),
            pltpu.VMEM((nx, 1, LANES), f32),
            pltpu.VMEM((ny, 1, LANES), f32),
            dma, dma, dma((3,)), dma, dma, dma((2,)), dma((4,)), dma((4,)), dma((3,)), dma((3,)),
        ],
        compiler_params=pltpu.CompilerParams(collective_id=0, has_side_effects=True),
        name="step",
    )(
        jnp.transpose(state, (0, 2, 1, 3)),
        patch_count,
        jnp.transpose(neighbour_table, (0, 2, 1)),
        jnp.transpose(send_table, (2, 0, 1)),
        jnp.transpose(ghost_table, (0, 2, 1)),
    )
    updated = kept - step[0, 0] * change
    return jnp.transpose(updated[None], (0, 2, 1, 3))


def solution(mesh):
    nx = ny = round((mesh.shape["morton"]) ** 0.5)
    sizes = (nx, ny, mesh.shape["group"] // 2, 2)
    torus = Mesh(mesh.devices.reshape(sizes), AXES)
    return jax.shard_map(
        functools.partial(per_device, sizes),
        mesh=torus,
        in_specs=(
            P(GROUP, MORTON, None, None),
            P(MORTON),
            P(MORTON, None, None),
            P(MORTON, None, None),
            P(MORTON, None, None),
        ),
        out_specs=P(GROUP, MORTON, None, None),
        check_vma=False,
    )
```

time: 169 us -> 38.7 us (0.23)
  the two profiles are of different devices: /device:TPU:2 before, /device:TPU:1 now
where the time goes in v1:
time: 38.7 us; the launch traced here: 38.5 us
  Pallas kernels  35.6 us (92%)
  other arithmetic  1.61 us (4%)
  between operations  0.67 us (2%)
  local copies, waits for them, and re-layouts  0.66 us (2%)
    pallas_call x1, Pallas kernels, per_device(): pl.pallas_call(functools.partial(kernel, sizes), out_shape=(jax.ShapeDtyp...  35.6 us
    transpose x1, other arithmetic, per_device(): return jnp.transpose(updated[None], (0, 2, 1, 3))  1.61 us

profile of v1, /device:TPU:1, one launch (start us, length us, event | category | flops | bytes accessed | tf_op | source)
XLA Modules:
  0.0 38.5 jit_solution(3229854076901327950)
XLA Ops:
  0.7 35.6 %step.1 = (f32[5,8,512]{2,1,0:T(8,128)}, f32[5,8,512]{2,1,0:T(8,128)}, f32[1,128]{1,0:T(1,128)}) custom-call(f32[1,5,8,512]{3,2,1,0:T(8,128)} %bitcast.10, s32[1]{0:T(128)S(6)} %copy.6.count, s32[1,4,8]{2,1,0:T(4,128)} %bitcast.12, s32[5,1,64]{2,1,0:T(1,128)} %bitcast.11, s32[1,4,8]{2,1,0:T(4,128)} %bitcast.13), custom_call_target="tpu_custom_call" | custom-call | tf_op jit(solution)/shard_map/step/pallas_call | solution.py:352
  36.2 0.0 copy-start
  36.2 0.7 %copy-done = f32[1,128]{1,0:T(1,128)S(1)} copy-done((f32[1,128]{1,0:T(1,128)S(1)}, f32[1,128]{1,0:T(1,128)}, u32[]{:S(2)}) %copy-start) | copy-done | bytes 536
  36.9 1.6 %subtract_bitcast_fusion = f32[1,8,5,512]{3,1,2,0:T(8,128)} fusion(f32[5,8,512]{2,1,0:T(8,128)} %get-tuple-element.8, f32[5,8,512]{2,1,0:T(8,128)} %get-tuple-element.10, f32[]{:T(128)S(1)} %bitcast.14), kind=kLoop, calls=%fused_computation | loop fusion | flops 40960 | bytes 245764 | tf_op jit(solution)/shard_map/transpose | solution.py:387
Async XLA Ops:
  36.2 0.7 %copy-start = (f32[1,128]{1,0:T(1,128)S(1)}, f32[1,128]{1,0:T(1,128)}, u32[]{:S(2)}) copy-start(f32[1,128]{1,0:T(1,128)} %get-tuple-element.9) | copy-start | bytes 1540

commit v2 on v1

--- a/solution.py
+++ b/solution.py
@@ -117,24 +117,31 @@
 def kernel(
     sizes,
     state, count, neighbour, send, ghost,
-    kept_out, change_out, top_out,
+    updated_out,
     cells_ref, count_ref, neighbour_ref, send_ref, ghost_ref,
-    vertical_out, vertical_in, lateral_out, lateral_in,
-    value, from_z, from_x, from_y,
+    vertical_out, vertical_in, lateral_out, lateral_in, change_ref,
+    value, from_plane, from_hubs, result,
     load_sem, count_sem, table_sem, up_sem, down_sem, vin_sem, lsend_sem, lin_sem, max_send, max_recv,
 ):
     nx, ny, nz, nc = sizes
     x, y, z, c = [lax.axis_index(a) for a in AXES]
     rank = x * ny + y
     ranks = nx * ny
+    in_plane = 2 * ny * nz
+    first = 2 * nx * ny
 
     def device(px, py, pz, pc):
         return {"morton_0": px, "morton_1": py, "group_0": pz, "group_1": pc}
+
+    def hub_of(px):
+        return device(px, 0, 0, HUB)
 
     def at_rank(offset):
         j = lax.rem(rank + (offset + ranks), ranks)
         return device(lax.div(j, ny), lax.rem(j, ny), z, c)
 
+    is_hub = (y == 0) & (z == 0) & (c == HUB)
+    is_first = z == 0
     other = 1 - c
     below = device(x, y, lax.rem(z + (nz - 1) + c, nz), other)
     above = device(x, y, lax.rem(z + c, nz), other)
@@ -154,32 +161,29 @@
     def greet(target):
         pl.semaphore_signal(barrier, inc=1, device_id=target, device_id_type=pl.DeviceIdType.MESH)
 
-    def on(axis_size, here, step):
-        return lax.rem(here + step, axis_size)
-
-    hub_partners = (nz - 1) + (nx - 1) + (ny - 1) * 2 + 1
     for target in [below, above] + [at_rank(o) for o in OFFSETS]:
         greet(target)
 
-    @pl.when(c == HUB)
-    def _():
-        for step in range(1, nz):
-            greet(device(x, y, on(nz, z, step), HUB))
-        for step in range(nz):
-            greet(device(x, y, on(nz, z, step), 1 - HUB))
+    @pl.when(is_hub)
+    def _():
         for step in range(1, nx):
-            greet(device(on(nx, x, step), y, z, HUB))
-        for step in range(1, ny):
-            greet(device(x, on(ny, y, step), z, HUB))
-
-    @pl.when(c != HUB)
-    def _():
-        for step in range(ny):
-            greet(device(x, on(ny, y, step), z, HUB))
+            greet(hub_of(lax.rem(x + step, nx)))
+        greet(device(x, 0, 0, 1 - HUB))
+
+        def plane(i, carry):
+            greet(device(x, lax.rem(lax.div(i, 2), ny), lax.div(i, 2 * ny), lax.rem(i, 2)))
+            return carry
+
+        lax.fori_loop(2, in_plane, plane, 0)
+
+    @pl.when(is_first & jnp.logical_not(is_hub))
+    def _():
+        for px in range(nx):
+            greet(hub_of(px))
 
     loads[1].wait()
     loads[0].wait()
-    live = lax.broadcasted_iota(jnp.int32, (SLOTS, CELLS), 0) < count_ref[0]
+    live = lax.broadcasted_iota(jnp.int32, (SLOTS, CELLS), 0) < jnp.broadcast_to(count_ref[...], (SLOTS, CELLS))
     cells = [cells_ref[v] for v in range(VARS)]
     prims = primitives(cells)
     velocity, pressure, sound = prims
@@ -188,33 +192,25 @@
     top = jnp.max(functools.reduce(jnp.maximum, tiles_of(speed)), axis=0, keepdims=True)
     value[0] = top
 
-    @pl.when(c == HUB)
-    def _():
-        from_z[z * 2 + HUB] = top
-        pl.semaphore_wait(barrier, hub_partners + 2 * 3)
-
-    @pl.when(c != HUB)
-    def _():
-        pl.semaphore_wait(barrier, nz + 2 * 3)
-
-    def push(source, target_ref, target, phase):
-        copy = pltpu.make_async_remote_copy(
-            src_ref=source, dst_ref=target_ref, send_sem=max_send.at[phase], recv_sem=max_recv.at[phase],
-            device_id=target, device_id_type=pl.DeviceIdType.MESH)
-        copy.start()
+    def push(source, target_ref, target, phase, arrival):
+        pltpu.make_async_remote_copy(
+            src_ref=source, dst_ref=target_ref, send_sem=max_send.at[phase], recv_sem=max_recv.at[arrival],
+            device_id=target, device_id_type=pl.DeviceIdType.MESH).start()
 
     def settle(ref, number, sem):
         pltpu.make_async_copy(ref.at[pl.ds(0, number)], ref.at[pl.ds(0, number)], sem).wait()
 
-    def highest(ref, number):
-        return functools.reduce(jnp.maximum, [ref[i] for i in range(number)])
-
-    for step in range(1, nz):
-        push(value.at[0], from_z.at[z * 2 + c], device(x, y, on(nz, z, step), HUB), 0)
-
-    @pl.when(c != HUB)
-    def _():
-        push(value.at[0], from_z.at[z * 2 + c], device(x, y, z, HUB), 0)
+    mine = (z * ny + y) * 2 + c
+
+    @pl.when(is_hub)
+    def _():
+        from_plane[mine] = top
+        pl.semaphore_wait(barrier, first - 1 + 2 * 3)
+
+    @pl.when(jnp.logical_not(is_hub))
+    def _():
+        pl.semaphore_wait(barrier, 1 + 2 * 3)
+        push(value.at[0], from_plane.at[mine], hub_of(x), 0, 0)
 
     vertical_out[0] = pack_face(cells, 4)
     vertical_out[1] = pack_face(cells, 5)
@@ -250,15 +246,6 @@
             device_id=at_rank(offset), device_id_type=pl.DeviceIdType.MESH)
         copy.start()
         lateral.append(copy)
-
-    @pl.when(c == HUB)
-    def _():
-        settle(from_z, 2 * nz - 1, max_recv.at[0])
-        along_z = highest(from_z, 2 * nz)
-        value[1] = along_z
-        from_x[x] = along_z
-        for step in range(1, nx):
-            push(value.at[1], from_x.at[x], device(on(nx, x, step), y, z, HUB), 1)
 
     loads[2].wait()
     loads[4].wait()
@@ -305,42 +292,65 @@
             total[v] = total[v] + 0.5 * (
                 (flux_high[v] - flux_low[v]) - (upper * (high[v] - cells[v]) - lower * (cells[v] - low[v])))
     for v in range(VARS):
-        kept_out[v] = jnp.where(live, cells[v], 0.0)
-        change_out[v] = jnp.where(live, total[v], 0.0)
-
-    @pl.when(c == HUB)
-    def _():
-        settle(from_x, nx - 1, max_recv.at[1])
-        plane = highest(from_x, nx)
-        value[2] = plane
-        from_y[y] = plane
-        push(value.at[2], from_y.at[y], device(x, y, z, 1 - HUB), 2)
-        for step in range(1, ny):
-            push(value.at[2], from_y.at[y], device(x, on(ny, y, step), z, HUB), 2)
-            push(value.at[2], from_y.at[y], device(x, on(ny, y, step), z, 1 - HUB), 2)
-        settle(from_y, ny - 1, max_recv.at[2])
-
-    @pl.when(c != HUB)
-    def _():
-        settle(from_y, ny, max_recv.at[2])
-
-    over_all = jnp.max(highest(from_y, ny), axis=1, keepdims=True)
-    top_out[...] = jnp.broadcast_to(COURANT / over_all, (1, LANES))
+        change_ref[v] = total[v]
 
     go_down.wait_send()
     go_up.wait_send()
     for copy in lateral:
         copy.wait_send()
 
-    @pl.when(c == HUB)
-    def _():
-        settle(from_z, nz - 1, max_send.at[0])
-        settle(from_x, nx - 1, max_send.at[1])
-        settle(from_z, 2 * ny - 1, max_send.at[2])
-
-    @pl.when(c != HUB)
-    def _():
-        settle(from_z, nz, max_send.at[0])
+    def finish(highest):
+        step = COURANT / jnp.max(highest, axis=1, keepdims=True)
+        for v in range(VARS):
+            updated_out[v] = jnp.where(live, cells_ref[v] - step * change_ref[v], 0.0)
+
+    def of_hubs():
+        return functools.reduce(jnp.maximum, [from_hubs[i] for i in range(nx)])
+
+    @pl.when(is_hub)
+    def _():
+        settle(from_plane, in_plane - 1, max_recv.at[0])
+        plane_top = jnp.max(from_plane[...], axis=0)
+        value[1] = plane_top
+        from_hubs[x] = plane_top
+
+        def tell(i, carry):
+            px, py, pc = lax.rem(lax.div(i, 2), nx), lax.div(i, 2 * nx), lax.rem(i + 1, 2)
+
+            @pl.when((px != x) | (py != 0) | (pc != HUB))
+            def _():
+                push(value.at[1], from_hubs.at[x], device(px, py, 0, pc), 1, 1)
+
+            return carry
+
+        lax.fori_loop(0, first, tell, 0)
+        settle(from_hubs, nx - 1, max_recv.at[1])
+        finish(of_hubs())
+        settle(from_plane, first - 1, max_send.at[1])
+
+    @pl.when(is_first & (c == HUB) & jnp.logical_not(is_hub))
+    def _():
+        settle(from_hubs, nx, max_recv.at[1])
+        finish(of_hubs())
+        settle(from_plane, 1, max_send.at[0])
+
+    @pl.when(is_first & (c != HUB))
+    def _():
+        settle(from_hubs, nx, max_recv.at[1])
+        over_all = of_hubs()
+        value[2] = over_all
+        for pz in range(1, nz):
+            for pc in (1, 0):
+                push(value.at[2], result.at[0], device(x, y, pz, pc), 2, 2)
+        finish(over_all)
+        settle(from_plane, 1, max_send.at[0])
+        settle(from_plane, 2 * (nz - 1), max_send.at[2])
+
+    @pl.when(jnp.logical_not(is_first))
+    def _():
+        settle(result, 1, max_recv.at[2])
+        finish(result[0])
+        settle(from_plane, 1, max_send.at[0])
 
 
 def per_device(sizes, state, patch_count, neighbour_table, send_table, ghost_table):
@@ -349,18 +359,14 @@
     vmem = pl.BlockSpec(memory_space=pltpu.VMEM)
     f32 = jnp.float32
     dma = pltpu.SemaphoreType.DMA
-    kept, change, step = pl.pallas_call(
+    updated = pl.pallas_call(
         functools.partial(kernel, sizes),
-        out_shape=(
-            jax.ShapeDtypeStruct((VARS, SLOTS, CELLS), f32),
-            jax.ShapeDtypeStruct((VARS, SLOTS, CELLS), f32),
-            jax.ShapeDtypeStruct((1, LANES), f32),
-        ),
+        out_shape=pltpu.VMEM((VARS, SLOTS, CELLS), f32),
         in_specs=[any_space] * 5,
-        out_specs=(vmem, vmem, vmem),
+        out_specs=vmem,
         scratch_shapes=[
             pltpu.VMEM((VARS, SLOTS, CELLS), f32),
-            pltpu.SMEM((1,), jnp.int32),
+            pltpu.VMEM((1, 1), jnp.int32),
             pltpu.VMEM((4, SLOTS), jnp.int32),
             pltpu.VMEM((MSG, 1, nx * ny), jnp.int32),
             pltpu.VMEM((4, SLOTS), jnp.int32),
@@ -368,22 +374,22 @@
             pltpu.VMEM((2, SLOTS, WIDE), f32),
             pltpu.VMEM((4, SLOTS, WIDE), f32),
             pltpu.VMEM((4, SLOTS, WIDE), f32),
+            pltpu.VMEM((VARS, SLOTS, CELLS), f32),
             pltpu.VMEM((3, 1, LANES), f32),
-            pltpu.VMEM((2 * max(nz, ny), 1, LANES), f32),
+            pltpu.VMEM((2 * ny * max(nz, nx), 1, LANES), f32),
             pltpu.VMEM((nx, 1, LANES), f32),
-            pltpu.VMEM((ny, 1, LANES), f32),
+            pltpu.VMEM((1, 1, LANES), f32),
             dma, dma, dma((3,)), dma, dma, dma((2,)), dma((4,)), dma((4,)), dma((3,)), dma((3,)),
         ],
         compiler_params=pltpu.CompilerParams(collective_id=0, has_side_effects=True),
         name="step",
     )(
         jnp.transpose(state, (0, 2, 1, 3)),
-        patch_count,
+        patch_count.reshape(1, 1),
         jnp.transpose(neighbour_table, (0, 2, 1)),
         jnp.transpose(send_table, (2, 0, 1)),
         jnp.transpose(ghost_table, (0, 2, 1)),
     )
-    updated = kept - step[0, 0] * change
     return jnp.transpose(updated[None], (0, 2, 1, 3))
 
 

time: 38.7 us -> 34.3 us (0.89)
  the two profiles are of different devices: /device:TPU:1 before, /device:TPU:112 now
where the time goes in v2:
time: 34.3 us; the launch traced here: 34.2 us
  Pallas kernels  32.9 us (96%)
  between operations  0.66 us (2%)
  local copies, waits for them, and re-layouts  0.64 us (2%)
    pallas_call x1, Pallas kernels, per_device(): pl.pallas_call(functools.partial(kernel, sizes), out_shape=pltpu.VMEM((VA...  32.9 us

profile of v2, /device:TPU:112, one launch (start us, length us, event | category | flops | bytes accessed | tf_op | source)
XLA Modules:
  0.0 34.2 jit_solution(14670069939600119376)
XLA Ops:
  0.7 32.9 %step.1 = f32[5,8,512]{2,1,0:T(8,128)S(1)} custom-call(f32[1,5,8,512]{3,2,1,0:T(8,128)} %bitcast.10, s32[1,1]{1,0:T(1,128)} %bitcast.8.count, s32[1,4,8]{2,1,0:T(4,128)} %bitcast.12, s32[5,1,64]{2,1,0:T(1,128)} %bitcast.11, s32[1,4,8]{2,1,0:T(4,128)} %bitcast.13), custom_call_target="tpu_custom_call" | custom-call | tf_op jit(solution)/shard_map/step/pallas_call | solution.py:362
  33.5 0.6 %copy.7 = f32[1,8,5,512]{3,1,2,0:T(8,128)} copy(f32[1,8,5,512]{3,1,2,0:T(8,128)S(1)} %bitcast.9) | data formatting | bytes 163840

commit v3 on v2

--- a/solution.py
+++ b/solution.py
@@ -116,39 +116,48 @@
 
 def kernel(
     sizes,
-    state, count, neighbour, send, ghost,
+    state, neighbour, send, ghost,
     updated_out,
-    cells_ref, count_ref, neighbour_ref, send_ref, ghost_ref,
+    cells_ref, neighbour_ref, send_ref, ghost_ref,
     vertical_out, vertical_in, lateral_out, lateral_in, change_ref,
     value, from_plane, from_hubs, result,
-    load_sem, count_sem, table_sem, up_sem, down_sem, vin_sem, lsend_sem, lin_sem, max_send, max_recv,
+    load_sem, table_sem, up_sem, down_sem, vin_sem, lsend_sem, lin_sem, max_send, max_recv,
 ):
     nx, ny, nz, nc = sizes
     x, y, z, c = [lax.axis_index(a) for a in AXES]
     rank = x * ny + y
     ranks = nx * ny
     in_plane = 2 * ny * nz
-    first = 2 * nx * ny
+    slab = z * nc + c
+    has_below, has_above = slab > 0, slab < nz * nc - 1
+    mid = ny // 2
+
+    def group_of(py):
+        return ((py * 4 >= ny) & (py * 4 <= 3 * ny)).astype(jnp.int32) if not isinstance(py, int) else int(ny <= py * 4 <= 3 * ny)
+
+    members = [[py for py in range(ny) if group_of(py) == g] for g in (0, 1)]
 
     def device(px, py, pz, pc):
         return {"morton_0": px, "morton_1": py, "group_0": pz, "group_1": pc}
 
-    def hub_of(px):
-        return device(px, 0, 0, HUB)
+    def hub_of(px, group):
+        return device(px, group * mid, 0, HUB)
 
     def at_rank(offset):
         j = lax.rem(rank + (offset + ranks), ranks)
         return device(lax.div(j, ny), lax.rem(j, ny), z, c)
 
-    is_hub = (y == 0) & (z == 0) & (c == HUB)
-    is_first = z == 0
+    group = group_of(y)
+    is_hub = ((y == 0) | (y == mid)) & (z == 0) & (c == HUB)
+    is_listener = (z == 0) & jnp.logical_not(is_hub)
+    is_teller = (z == 1) & (c != HUB)
+    is_other = (z > 1) | ((z == 1) & (c == HUB))
     other = 1 - c
     below = device(x, y, lax.rem(z + (nz - 1) + c, nz), other)
     above = device(x, y, lax.rem(z + c, nz), other)
 
     loads = [
         pltpu.make_async_copy(state.at[0], cells_ref, load_sem),
-        pltpu.make_async_copy(count, count_ref, count_sem),
         pltpu.make_async_copy(neighbour.at[0], neighbour_ref, table_sem.at[0]),
         pltpu.make_async_copy(send, send_ref, table_sem.at[1]),
         pltpu.make_async_copy(ghost.at[0], ghost_ref, table_sem.at[2]),
@@ -161,29 +170,42 @@
     def greet(target):
         pl.semaphore_signal(barrier, inc=1, device_id=target, device_id_type=pl.DeviceIdType.MESH)
 
-    for target in [below, above] + [at_rank(o) for o in OFFSETS]:
+    for target in [at_rank(o) for o in OFFSETS]:
         greet(target)
 
+    @pl.when(has_below)
+    def _():
+        greet(below)
+
+    @pl.when(has_above)
+    def _():
+        greet(above)
+
     @pl.when(is_hub)
     def _():
+        def plane(i, carry):
+            py, pz, pc = lax.rem(lax.div(i, 2), ny), lax.div(i, 2 * ny), lax.rem(i, 2)
+
+            @pl.when((py != y) | (pz != 0) | (pc != HUB))
+            def _():
+                greet(device(x, py, pz, pc))
+
+            return carry
+
+        lax.fori_loop(0, in_plane, plane, 0)
         for step in range(1, nx):
-            greet(hub_of(lax.rem(x + step, nx)))
-        greet(device(x, 0, 0, 1 - HUB))
-
-        def plane(i, carry):
-            greet(device(x, lax.rem(lax.div(i, 2), ny), lax.div(i, 2 * ny), lax.rem(i, 2)))
-            return carry
-
-        lax.fori_loop(2, in_plane, plane, 0)
-
-    @pl.when(is_first & jnp.logical_not(is_hub))
+            greet(hub_of(lax.rem(x + step, nx), group))
+
+    @pl.when(is_listener | is_teller)
     def _():
         for px in range(nx):
-            greet(hub_of(px))
+            greet(hub_of(px, group))
 
     loads[1].wait()
+    near = neighbour_ref[...]
     loads[0].wait()
-    live = lax.broadcasted_iota(jnp.int32, (SLOTS, CELLS), 0) < jnp.broadcast_to(count_ref[...], (SLOTS, CELLS))
+    in_row = diagonal(jnp.maximum(near[2:3, :], near[3:4, :]).astype(jnp.float32))
+    live = jnp.broadcast_to(in_row, (SLOTS, CELLS)) >= 0.0
     cells = [cells_ref[v] for v in range(VARS)]
     prims = primitives(cells)
     velocity, pressure, sound = prims
@@ -202,15 +224,20 @@
 
     mine = (z * ny + y) * 2 + c
 
+    halo = 4 + has_below.astype(jnp.int32) + has_above.astype(jnp.int32)
+
     @pl.when(is_hub)
     def _():
         from_plane[mine] = top
-        pl.semaphore_wait(barrier, first - 1 + 2 * 3)
+        told = jnp.where(group == 0, len(members[0]), len(members[1])) * nx * 3
+        pl.semaphore_wait(barrier, told + halo)
+        push(value.at[0], from_plane.at[mine], hub_of(x, 1 - group), 0, 0)
 
     @pl.when(jnp.logical_not(is_hub))
     def _():
-        pl.semaphore_wait(barrier, 1 + 2 * 3)
-        push(value.at[0], from_plane.at[mine], hub_of(x), 0, 0)
+        pl.semaphore_wait(barrier, 2 + halo)
+        push(value.at[0], from_plane.at[mine], hub_of(x, 0), 0, 0)
+        push(value.at[0], from_plane.at[mine], hub_of(x, 1), 0, 0)
 
     vertical_out[0] = pack_face(cells, 4)
     vertical_out[1] = pack_face(cells, 5)
@@ -220,12 +247,27 @@
     go_up = pltpu.make_async_remote_copy(
         src_ref=vertical_out.at[1], dst_ref=vertical_in.at[0], send_sem=up_sem, recv_sem=vin_sem.at[0],
         device_id=above, device_id_type=pl.DeviceIdType.MESH)
-    go_down.start()
-    go_up.start()
+
+    @pl.when(has_below)
+    def _():
+        go_down.start()
+
+    @pl.when(jnp.logical_not(has_below))
+    def _():
+        vertical_in[0] = vertical_out[0]
+
+    @pl.when(has_above)
+    def _():
+        go_up.start()
+
+    @pl.when(jnp.logical_not(has_above))
+    def _():
+        vertical_in[1] = vertical_out[1]
+
 
     own = [pack_face(cells, face) for face in range(4)]
     own_rows = jnp.concatenate(own, axis=0)
-    loads[3].wait()
+    loads[2].wait()
     rows = jnp.concatenate([send_ref[t] for t in range(MSG)] + [jnp.full((SLOTS - MSG, ranks), -1, jnp.int32)], axis=0)
     columns = []
     for offset in OFFSETS:
@@ -247,16 +289,21 @@
         copy.start()
         lateral.append(copy)
 
-    loads[2].wait()
-    loads[4].wait()
-    go_down.wait_recv()
-    go_up.wait_recv()
+    loads[3].wait()
+
+    @pl.when(has_above)
+    def _():
+        go_down.wait_recv()
+
+    @pl.when(has_below)
+    def _():
+        go_up.wait_recv()
+
     for d in range(4):
         pltpu.make_async_remote_copy(
             src_ref=lateral_out.at[d], dst_ref=lateral_in.at[d], send_sem=lsend_sem.at[d], recv_sem=lin_sem.at[d],
             device_id=at_rank(1), device_id_type=pl.DeviceIdType.MESH).wait_recv()
     faces = jnp.concatenate([own_rows] + [lateral_in[d] for d in range(4)], axis=0)
-    near = neighbour_ref[...]
     far = ghost_ref[...]
     face_id = lax.broadcasted_iota(jnp.int32, (4, SLOTS), 0)
     slot_id = lane((4, SLOTS))
@@ -270,9 +317,8 @@
     hot = one_hot(jnp.concatenate(columns, axis=0), 8 * SLOTS)
     chosen = select_rows(hot, faces)
     ghosts = [chosen[k * SLOTS:(k + 1) * SLOTS] for k in range(4)]
-    slab = z * nc + c
-    ghosts.append(jnp.where(slab == 0, vertical_out[0], vertical_in[0]))
-    ghosts.append(jnp.where(slab == nz * nc - 1, vertical_out[1], vertical_in[1]))
+    ghosts.append(vertical_in[0])
+    ghosts.append(vertical_in[1])
 
     total = [0.0] * VARS
     at = lane((SLOTS, CELLS))
@@ -294,8 +340,14 @@
     for v in range(VARS):
         change_ref[v] = total[v]
 
-    go_down.wait_send()
-    go_up.wait_send()
+    @pl.when(has_below)
+    def _():
+        go_down.wait_send()
+
+    @pl.when(has_above)
+    def _():
+        go_up.wait_send()
+
     for copy in lateral:
         copy.wait_send()
 
@@ -307,50 +359,57 @@
     def of_hubs():
         return functools.reduce(jnp.maximum, [from_hubs[i] for i in range(nx)])
 
-    @pl.when(is_hub)
-    def _():
-        settle(from_plane, in_plane - 1, max_recv.at[0])
-        plane_top = jnp.max(from_plane[...], axis=0)
-        value[1] = plane_top
-        from_hubs[x] = plane_top
-
-        def tell(i, carry):
-            px, py, pc = lax.rem(lax.div(i, 2), nx), lax.div(i, 2 * nx), lax.rem(i + 1, 2)
-
-            @pl.when((px != x) | (py != 0) | (pc != HUB))
-            def _():
-                push(value.at[1], from_hubs.at[x], device(px, py, 0, pc), 1, 1)
-
-            return carry
-
-        lax.fori_loop(0, first, tell, 0)
-        settle(from_hubs, nx - 1, max_recv.at[1])
-        finish(of_hubs())
-        settle(from_plane, first - 1, max_send.at[1])
-
-    @pl.when(is_first & (c == HUB) & jnp.logical_not(is_hub))
+    for g in (0, 1):
+        number = len(members[g]) * nx * 3 - 1
+
+        @pl.when(is_hub & (group == g))
+        def _(g=g, number=number):
+            settle(from_plane, in_plane - 1, max_recv.at[0])
+            plane_top = jnp.max(from_plane[pl.ds(0, in_plane)], axis=0)
+            value[1] = plane_top
+            from_hubs[x] = plane_top
+
+            def tell(i, carry):
+                py = i + members[1][0] if g else jnp.where(i < members[1][0], i, i + len(members[1]))
+                for px in range(nx):
+                    @pl.when((px != x) | (py != y))
+                    def _(px=px):
+                        push(value.at[1], from_hubs.at[x], device(px, py, 0, HUB), 1, 1)
+
+                    push(value.at[1], from_hubs.at[x], device(px, py, 0, 1 - HUB), 1, 1)
+                    push(value.at[1], from_hubs.at[x], device(px, py, 1, 1 - HUB), 1, 1)
+                return carry
+
+            lax.fori_loop(0, len(members[g]), tell, 0)
+            settle(from_hubs, nx - 1, max_recv.at[1])
+            finish(of_hubs())
+            settle(from_plane, 1, max_send.at[0])
+            settle(from_plane, number, max_send.at[1])
+
+    @pl.when(is_listener)
     def _():
         settle(from_hubs, nx, max_recv.at[1])
         finish(of_hubs())
-        settle(from_plane, 1, max_send.at[0])
-
-    @pl.when(is_first & (c != HUB))
+        settle(from_plane, 2, max_send.at[0])
+
+    @pl.when(is_teller)
     def _():
         settle(from_hubs, nx, max_recv.at[1])
         over_all = of_hubs()
         value[2] = over_all
-        for pz in range(1, nz):
+        push(value.at[2], result.at[0], device(x, y, 1, HUB), 2, 2)
+        for pz in range(2, nz):
             for pc in (1, 0):
                 push(value.at[2], result.at[0], device(x, y, pz, pc), 2, 2)
         finish(over_all)
-        settle(from_plane, 1, max_send.at[0])
-        settle(from_plane, 2 * (nz - 1), max_send.at[2])
-
-    @pl.when(jnp.logical_not(is_first))
+        settle(from_plane, 2, max_send.at[0])
+        settle(from_plane, 2 * nz - 3, max_send.at[2])
+
+    @pl.when(is_other)
     def _():
         settle(result, 1, max_recv.at[2])
         finish(result[0])
-        settle(from_plane, 1, max_send.at[0])
+        settle(from_plane, 2, max_send.at[0])
 
 
 def per_device(sizes, state, patch_count, neighbour_table, send_table, ghost_table):
@@ -362,11 +421,10 @@
     updated = pl.pallas_call(
         functools.partial(kernel, sizes),
         out_shape=pltpu.VMEM((VARS, SLOTS, CELLS), f32),
-        in_specs=[any_space] * 5,
+        in_specs=[any_space] * 4,
         out_specs=vmem,
         scratch_shapes=[
             pltpu.VMEM((VARS, SLOTS, CELLS), f32),
-            pltpu.VMEM((1, 1), jnp.int32),
             pltpu.VMEM((4, SLOTS), jnp.int32),
             pltpu.VMEM((MSG, 1, nx * ny), jnp.int32),
             pltpu.VMEM((4, SLOTS), jnp.int32),
@@ -376,16 +434,15 @@
             pltpu.VMEM((4, SLOTS, WIDE), f32),
             pltpu.VMEM((VARS, SLOTS, CELLS), f32),
             pltpu.VMEM((3, 1, LANES), f32),
-            pltpu.VMEM((2 * ny * max(nz, nx), 1, LANES), f32),
+            pltpu.VMEM((max(2 * ny * nz, 3 * nx * ny), 1, LANES), f32),
             pltpu.VMEM((nx, 1, LANES), f32),
             pltpu.VMEM((1, 1, LANES), f32),
-            dma, dma, dma((3,)), dma, dma, dma((2,)), dma((4,)), dma((4,)), dma((3,)), dma((3,)),
+            dma, dma((3,)), dma, dma, dma((2,)), dma((4,)), dma((4,)), dma((3,)), dma((3,)),
         ],
         compiler_params=pltpu.CompilerParams(collective_id=0, has_side_effects=True),
         name="step",
     )(
         jnp.transpose(state, (0, 2, 1, 3)),
-        patch_count.reshape(1, 1),
         jnp.transpose(neighbour_table, (0, 2, 1)),
         jnp.transpose(send_table, (2, 0, 1)),
         jnp.transpose(ghost_table, (0, 2, 1)),

time: 34.3 us -> 32.6 us (0.950)
  the two profiles are of different devices: /device:TPU:112 before, /device:TPU:1 now
where the time goes in v3:
time: 32.6 us; the launch traced here: 32.4 us
  Pallas kernels  31.8 us (98%)
  local copies, waits for them, and re-layouts  0.64 us (2%)
    pallas_call x1, Pallas kernels, per_device(): pl.pallas_call(functools.partial(kernel, sizes), out_shape=pltpu.VMEM((VA...  31.8 us

profile of v3, /device:TPU:1, one launch (start us, length us, event | category | flops | bytes accessed | tf_op | source)
XLA Modules:
  0.0 32.4 jit_solution(7346127520360460262)
XLA Ops:
  0.0 31.8 %step.1 = f32[5,8,512]{2,1,0:T(8,128)S(1)} custom-call(f32[1,5,8,512]{3,2,1,0:T(8,128)} %bitcast.8, s32[1,4,8]{2,1,0:T(4,128)} %bitcast.10, s32[5,1,64]{2,1,0:T(1,128)} %bitcast.9, s32[1,4,8]{2,1,0:T(4,128)} %bitcast.11), custom_call_target="tpu_custom_call" | custom-call | tf_op jit(solution)/shard_map/step/pallas_call | solution.py:421
  31.8 0.6 %copy.6 = f32[1,8,5,512]{3,1,2,0:T(8,128)} copy(f32[1,8,5,512]{3,1,2,0:T(8,128)S(1)} %bitcast.7) | data formatting | bytes 163840

commit v4 on v3

--- a/solution.py
+++ b/solution.py
@@ -114,13 +114,20 @@
     return jnp.dot(hot, table, precision=lax.Precision.HIGHEST, preferred_element_type=jnp.float32)
 
 
+def late_sets(sizes):
+    nx, ny, nz, nc = sizes
+    late_x = [px for px in range(nx) if abs(px - nx // 2) <= nx // 8]
+    late_y = [py for py in range(ny) if abs(py - ny // 2) <= ny // 4]
+    return late_x, late_y, nz - nz // 2
+
+
 def kernel(
     sizes,
     state, neighbour, send, ghost,
     updated_out,
     cells_ref, neighbour_ref, send_ref, ghost_ref,
     vertical_out, vertical_in, lateral_out, lateral_in, change_ref,
-    value, from_plane, from_hubs, result,
+    value, from_plane, from_late, from_hubs, direct, result,
     load_sem, table_sem, up_sem, down_sem, vin_sem, lsend_sem, lin_sem, max_send, max_recv,
 ):
     nx, ny, nz, nc = sizes
@@ -132,10 +139,9 @@
     has_below, has_above = slab > 0, slab < nz * nc - 1
     mid = ny // 2
 
-    def group_of(py):
-        return ((py * 4 >= ny) & (py * 4 <= 3 * ny)).astype(jnp.int32) if not isinstance(py, int) else int(ny <= py * 4 <= 3 * ny)
-
-    members = [[py for py in range(ny) if group_of(py) == g] for g in (0, 1)]
+    members = [[0], list(range(1, ny))]
+    late_x, late_y, late_z = late_sets(sizes)
+    n_late = len(late_y) * late_z * 2
 
     def device(px, py, pz, pc):
         return {"morton_0": px, "morton_1": py, "group_0": pz, "group_1": pc}
@@ -147,7 +153,27 @@
         j = lax.rem(rank + (offset + ranks), ranks)
         return device(lax.div(j, ny), lax.rem(j, ny), z, c)
 
-    group = group_of(y)
+    group = jnp.minimum(y, 1)
+
+    def is_late(px, py, pz):
+        return (px >= late_x[0]) & (px <= late_x[-1]) & (py >= late_y[0]) & (py <= late_y[-1]) & (pz >= nz - late_z)
+
+    late = is_late(x, y, z)
+    late_plane = (x >= late_x[0]) & (x <= late_x[-1])
+    first_device = device(0, 0, 0, HUB)
+    is_first_device = (x == 0) & (y == 0) & (z == 0) & (c == HUB)
+
+    def key(px, py, pz, pc):
+        hops = jnp.minimum(px, nx - px) + jnp.minimum(py, ny - py) + jnp.minimum(pz, nz - pz)
+        far = lax.div(2 * px, nx) + lax.div(2 * py, ny) + lax.div(2 * pz, nz)
+        number = ((pz * ny + py) * nx + px) * 2 + pc
+        return (14 * number + 443 * hops + 620 * far - 420 * pc) * (2 * nx * ny * nz) + number
+
+    my_key = key(x, y, z, c)
+
+    def comes_later(p):
+        return key(p["morton_0"], p["morton_1"], p["group_0"], p["group_1"]) > my_key
+
     is_hub = ((y == 0) | (y == mid)) & (z == 0) & (c == HUB)
     is_listener = (z == 0) & jnp.logical_not(is_hub)
     is_teller = (z == 1) & (c != HUB)
@@ -157,7 +183,8 @@
     above = device(x, y, lax.rem(z + c, nz), other)
 
     loads = [
-        pltpu.make_async_copy(state.at[0], cells_ref, load_sem),
+        pltpu.make_async_copy(state.at[0, v], cells_ref.at[v], load_sem.at[v]) for v in range(VARS)
+    ] + [
         pltpu.make_async_copy(neighbour.at[0], neighbour_ref, table_sem.at[0]),
         pltpu.make_async_copy(send, send_ref, table_sem.at[1]),
         pltpu.make_async_copy(ghost.at[0], ghost_ref, table_sem.at[2]),
@@ -170,16 +197,19 @@
     def greet(target):
         pl.semaphore_signal(barrier, inc=1, device_id=target, device_id_type=pl.DeviceIdType.MESH)
 
-    for target in [at_rank(o) for o in OFFSETS]:
-        greet(target)
-
-    @pl.when(has_below)
-    def _():
-        greet(below)
-
-    @pl.when(has_above)
-    def _():
-        greet(above)
+    beside = [at_rank(o) for o in OFFSETS]
+    beside_later = [comes_later(p) for p in beside]
+    below_later, above_later = has_below & comes_later(below), has_above & comes_later(above)
+    below_earlier = has_below & jnp.logical_not(below_later)
+    above_earlier = has_above & jnp.logical_not(above_later)
+    partners = list(zip(beside + [below, above], beside_later + [below_later, above_later]))
+    earlier = sum(jnp.logical_not(f).astype(jnp.int32) for f in beside_later)
+    earlier = earlier + below_earlier.astype(jnp.int32) + above_earlier.astype(jnp.int32)
+
+    for target, later in partners:
+        @pl.when(later)
+        def _(target=target):
+            greet(target)
 
     @pl.when(is_hub)
     def _():
@@ -196,14 +226,25 @@
         for step in range(1, nx):
             greet(hub_of(lax.rem(x + step, nx), group))
 
+    @pl.when(is_first_device)
+    def _():
+        def late_one(i, carry):
+            px = late_x[0] + lax.rem(lax.div(i, 2), len(late_x))
+            rest = lax.div(i, 2 * len(late_x))
+            greet(device(px, late_y[0] + lax.rem(rest, len(late_y)), nz - late_z + lax.div(rest, len(late_y)), lax.rem(i, 2)))
+            return carry
+
+        lax.fori_loop(0, len(late_x) * n_late, late_one, 0)
+
     @pl.when(is_listener | is_teller)
     def _():
         for px in range(nx):
             greet(hub_of(px, group))
 
-    loads[1].wait()
+    loads[VARS].wait()
     near = neighbour_ref[...]
-    loads[0].wait()
+    for v in range(VARS):
+        loads[v].wait()
     in_row = diagonal(jnp.maximum(near[2:3, :], near[3:4, :]).astype(jnp.float32))
     live = jnp.broadcast_to(in_row, (SLOTS, CELLS)) >= 0.0
     cells = [cells_ref[v] for v in range(VARS)]
@@ -222,22 +263,35 @@
     def settle(ref, number, sem):
         pltpu.make_async_copy(ref.at[pl.ds(0, number)], ref.at[pl.ds(0, number)], sem).wait()
 
-    mine = (z * ny + y) * 2 + c
-
-    halo = 4 + has_below.astype(jnp.int32) + has_above.astype(jnp.int32)
+    packed_z, others = z - (nz - late_z), ny - len(late_y)
+    packed_y = jnp.where(y < late_y[0], y, y - len(late_y))
+    mine = jnp.where(
+        late_plane & (packed_z >= 0),
+        ((nz - late_z) * ny + packed_z * others + packed_y) * 2 + c,
+        (z * ny + y) * 2 + c,
+    )
+
 
     @pl.when(is_hub)
     def _():
         from_plane[mine] = top
         told = jnp.where(group == 0, len(members[0]), len(members[1])) * nx * 3
-        pl.semaphore_wait(barrier, told + halo)
+        pl.semaphore_wait(barrier, told + earlier)
         push(value.at[0], from_plane.at[mine], hub_of(x, 1 - group), 0, 0)
 
-    @pl.when(jnp.logical_not(is_hub))
-    def _():
-        pl.semaphore_wait(barrier, 2 + halo)
+    @pl.when(late)
+    def _():
+        place = ((z - (nz - late_z)) * len(late_y) + y - late_y[0]) * 2 + c
+        pl.semaphore_wait(barrier, 3 + earlier)
+        push(value.at[0], direct.at[(x - late_x[0]) * n_late + place], first_device, 0, 4)
+        push(value.at[0], from_late.at[place], hub_of(x, 1), 0, 3)
+        push(value.at[0], from_late.at[place], hub_of(x, 0), 0, 3)
+
+    @pl.when(jnp.logical_not(is_hub | late))
+    def _():
+        pl.semaphore_wait(barrier, 2 + earlier)
+        push(value.at[0], from_plane.at[mine], hub_of(x, 1), 0, 0)
         push(value.at[0], from_plane.at[mine], hub_of(x, 0), 0, 0)
-        push(value.at[0], from_plane.at[mine], hub_of(x, 1), 0, 0)
 
     vertical_out[0] = pack_face(cells, 4)
     vertical_out[1] = pack_face(cells, 5)
@@ -248,26 +302,25 @@
         src_ref=vertical_out.at[1], dst_ref=vertical_in.at[0], send_sem=up_sem, recv_sem=vin_sem.at[0],
         device_id=above, device_id_type=pl.DeviceIdType.MESH)
 
-    @pl.when(has_below)
+    @pl.when(below_earlier)
     def _():
         go_down.start()
 
+    @pl.when(above_earlier)
+    def _():
+        go_up.start()
+
     @pl.when(jnp.logical_not(has_below))
     def _():
         vertical_in[0] = vertical_out[0]
 
-    @pl.when(has_above)
-    def _():
-        go_up.start()
-
     @pl.when(jnp.logical_not(has_above))
     def _():
         vertical_in[1] = vertical_out[1]
-
 
     own = [pack_face(cells, face) for face in range(4)]
     own_rows = jnp.concatenate(own, axis=0)
-    loads[2].wait()
+    loads[VARS + 1].wait()
     rows = jnp.concatenate([send_ref[t] for t in range(MSG)] + [jnp.full((SLOTS - MSG, ranks), -1, jnp.int32)], axis=0)
     columns = []
     for offset in OFFSETS:
@@ -281,28 +334,51 @@
     messages = select_rows(hot, own_rows)
     for d in range(4):
         lateral_out[d] = messages[d * SLOTS:(d + 1) * SLOTS]
-    lateral = []
-    for d, offset in enumerate(OFFSETS):
-        copy = pltpu.make_async_remote_copy(
-            src_ref=lateral_out.at[d], dst_ref=lateral_in.at[3 - d], send_sem=lsend_sem.at[d], recv_sem=lin_sem.at[3 - d],
-            device_id=at_rank(offset), device_id_type=pl.DeviceIdType.MESH)
-        copy.start()
-        lateral.append(copy)
-
-    loads[3].wait()
-
-    @pl.when(has_above)
+    lateral = [pltpu.make_async_remote_copy(
+        src_ref=lateral_out.at[d], dst_ref=lateral_in.at[3 - d], send_sem=lsend_sem.at[d], recv_sem=lin_sem.at[3 - d],
+        device_id=beside[d], device_id_type=pl.DeviceIdType.MESH) for d in range(4)]
+
+    def arrived(d):
+        return pltpu.make_async_remote_copy(
+            src_ref=lateral_out.at[d], dst_ref=lateral_in.at[d], send_sem=lsend_sem.at[d], recv_sem=lin_sem.at[d],
+            device_id=beside[d], device_id_type=pl.DeviceIdType.MESH)
+
+    for d in range(4):
+        @pl.when(jnp.logical_not(beside_later[d]))
+        def _(d=d):
+            lateral[d].start()
+
+    for d in range(4):
+        @pl.when(beside_later[d])
+        def _(d=d):
+            arrived(d).wait_recv()
+            lateral[d].start()
+
+    @pl.when(below_later)
+    def _():
+        go_up.wait_recv()
+        go_down.start()
+
+    @pl.when(above_later)
     def _():
         go_down.wait_recv()
-
-    @pl.when(has_below)
+        go_up.start()
+
+    loads[VARS + 2].wait()
+
+    for d in range(4):
+        @pl.when(jnp.logical_not(beside_later[d]))
+        def _(d=d):
+            arrived(d).wait_recv()
+
+    @pl.when(above_earlier)
+    def _():
+        go_down.wait_recv()
+
+    @pl.when(below_earlier)
     def _():
         go_up.wait_recv()
 
-    for d in range(4):
-        pltpu.make_async_remote_copy(
-            src_ref=lateral_out.at[d], dst_ref=lateral_in.at[d], send_sem=lsend_sem.at[d], recv_sem=lin_sem.at[d],
-            device_id=at_rank(1), device_id_type=pl.DeviceIdType.MESH).wait_recv()
     faces = jnp.concatenate([own_rows] + [lateral_in[d] for d in range(4)], axis=0)
     far = ghost_ref[...]
     face_id = lax.broadcasted_iota(jnp.int32, (4, SLOTS), 0)
@@ -359,20 +435,38 @@
     def of_hubs():
         return functools.reduce(jnp.maximum, [from_hubs[i] for i in range(nx)])
 
+    def plane_top_of(rows):
+        return jnp.max(from_plane[pl.ds(0, rows)], axis=0)
+
     for g in (0, 1):
         number = len(members[g]) * nx * 3 - 1
 
         @pl.when(is_hub & (group == g))
         def _(g=g, number=number):
-            settle(from_plane, in_plane - 1, max_recv.at[0])
-            plane_top = jnp.max(from_plane[pl.ds(0, in_plane)], axis=0)
-            value[1] = plane_top
-            from_hubs[x] = plane_top
+            @pl.when(jnp.logical_not(late_plane))
+            def _():
+                settle(from_plane, in_plane - 1, max_recv.at[0])
+                value[1] = plane_top_of(in_plane)
+
+            @pl.when(late_plane)
+            def _():
+                settle(from_plane, in_plane - n_late - 1, max_recv.at[0])
+                value[2] = plane_top_of(in_plane - n_late)
+                if g == 0:
+                    push(value.at[2], from_hubs.at[x], first_device, 2, 1)
+                settle(from_late, n_late, max_recv.at[3])
+                value[1] = jnp.maximum(value[2], jnp.max(from_late[...], axis=0))
+
+            from_hubs[x] = value[1]
 
             def tell(i, carry):
-                py = i + members[1][0] if g else jnp.where(i < members[1][0], i, i + len(members[1]))
+                py = i + members[g][0]
                 for px in range(nx):
-                    @pl.when((px != x) | (py != y))
+                    unless = (px != x) | (py != y)
+                    if g == 0 and px == 0:
+                        unless = unless & jnp.logical_not(late_plane)
+
+                    @pl.when(unless)
                     def _(px=px):
                         push(value.at[1], from_hubs.at[x], device(px, py, 0, HUB), 1, 1)
 
@@ -382,15 +476,33 @@
 
             lax.fori_loop(0, len(members[g]), tell, 0)
             settle(from_hubs, nx - 1, max_recv.at[1])
-            finish(of_hubs())
+            if g == 0:
+                @pl.when(is_first_device)
+                def _():
+                    settle(direct, len(late_x) * n_late, max_recv.at[4])
+                    finish(jnp.maximum(of_hubs(), jnp.max(direct[...], axis=0)))
+
+                @pl.when(jnp.logical_not(is_first_device))
+                def _():
+                    finish(of_hubs())
+
+                @pl.when(late_plane)
+                def _():
+                    settle(from_plane, 1, max_send.at[2])
+                    settle(from_plane, number - 1, max_send.at[1])
+
+                @pl.when(jnp.logical_not(late_plane))
+                def _():
+                    settle(from_plane, number, max_send.at[1])
+            else:
+                finish(of_hubs())
+                settle(from_plane, number, max_send.at[1])
             settle(from_plane, 1, max_send.at[0])
-            settle(from_plane, number, max_send.at[1])
 
     @pl.when(is_listener)
     def _():
         settle(from_hubs, nx, max_recv.at[1])
         finish(of_hubs())
-        settle(from_plane, 2, max_send.at[0])
 
     @pl.when(is_teller)
     def _():
@@ -402,18 +514,26 @@
             for pc in (1, 0):
                 push(value.at[2], result.at[0], device(x, y, pz, pc), 2, 2)
         finish(over_all)
-        settle(from_plane, 2, max_send.at[0])
         settle(from_plane, 2 * nz - 3, max_send.at[2])
 
     @pl.when(is_other)
     def _():
         settle(result, 1, max_recv.at[2])
         finish(result[0])
+
+    @pl.when(late)
+    def _():
+        settle(from_plane, 3, max_send.at[0])
+
+    @pl.when(jnp.logical_not(is_hub | late))
+    def _():
         settle(from_plane, 2, max_send.at[0])
 
 
 def per_device(sizes, state, patch_count, neighbour_table, send_table, ghost_table):
     nx, ny, nz, nc = sizes
+    late_x, late_y, late_z = late_sets(sizes)
+    n_late = len(late_y) * late_z * 2
     any_space = pl.BlockSpec(memory_space=pl.ANY)
     vmem = pl.BlockSpec(memory_space=pltpu.VMEM)
     f32 = jnp.float32
@@ -435,9 +555,11 @@
             pltpu.VMEM((VARS, SLOTS, CELLS), f32),
             pltpu.VMEM((3, 1, LANES), f32),
             pltpu.VMEM((max(2 * ny * nz, 3 * nx * ny), 1, LANES), f32),
+            pltpu.VMEM((n_late, 1, LANES), f32),
             pltpu.VMEM((nx, 1, LANES), f32),
+            pltpu.VMEM((len(late_x) * n_late, 1, LANES), f32),
             pltpu.VMEM((1, 1, LANES), f32),
-            dma, dma((3,)), dma, dma, dma((2,)), dma((4,)), dma((4,)), dma((3,)), dma((3,)),
+            dma((VARS,)), dma((3,)), dma, dma, dma((2,)), dma((4,)), dma((4,)), dma((3,)), dma((5,)),
         ],
         compiler_params=pltpu.CompilerParams(collective_id=0, has_side_effects=True),
         name="step",

time: 32.6 us -> 31.5 us (0.966)
  Pallas kernels: 31.8 us -> 30.7 us
    pallas_call x1, Pallas kernels: 31.8 us -> 30.7 us  [per_device(): pl.pallas_call(functools.partial(kernel, sizes), out_shape=pltpu.VMEM((VA...]
where the time goes in v4:
time: 31.5 us; the launch traced here: 31.4 us
  Pallas kernels  30.7 us (97%)
  local copies, waits for them, and re-layouts  0.64 us (2%)
    pallas_call x1, Pallas kernels, per_device(): pl.pallas_call(functools.partial(kernel, sizes), out_shape=pltpu.VMEM((VA...  30.7 us
    unnamed x1, local copies, waits for them, and re-layouts  0.64 us

profile of v4, /device:TPU:1, one launch (start us, length us, event | category | flops | bytes accessed | tf_op | source)
XLA Modules:
  0.0 31.4 jit_solution(1359409824157968588)
XLA Ops:
  0.0 30.7 %step.1 = f32[5,8,512]{2,1,0:T(8,128)S(1)} custom-call(f32[1,5,8,512]{3,2,1,0:T(8,128)} %bitcast.8, s32[1,4,8]{2,1,0:T(4,128)} %bitcast.10, s32[5,1,64]{2,1,0:T(1,128)} %bitcast.9, s32[1,4,8]{2,1,0:T(4,128)} %bitcast.11), custom_call_target="tpu_custom_call" | custom-call | tf_op jit(solution)/shard_map/step/pallas_call | solution.py:541
  30.7 0.6 %copy.6 = f32[1,8,5,512]{3,1,2,0:T(8,128)} copy(f32[1,8,5,512]{3,1,2,0:T(8,128)S(1)} %bitcast.7) | data formatting | bytes 163840

commit v5 on v4

--- a/solution.py
+++ b/solution.py
@@ -114,20 +114,20 @@
     return jnp.dot(hot, table, precision=lax.Precision.HIGHEST, preferred_element_type=jnp.float32)
 
 
-def late_sets(sizes):
+def early_and_late(sizes):
     nx, ny, nz, nc = sizes
-    late_x = [px for px in range(nx) if abs(px - nx // 2) <= nx // 8]
-    late_y = [py for py in range(ny) if abs(py - ny // 2) <= ny // 4]
-    return late_x, late_y, nz - nz // 2
+    late_x = [px for px in range(nx) if abs(px - nx // 2) <= nx // 4]
+    early = [(0, 0, HUB)] + [(px, py, pc) for px, py in ((1, 0), (0, 1)) for pc in (HUB, 1 - HUB) if px not in late_x]
+    return early, late_x, nz - nz // 2
 
 
 def kernel(
     sizes,
     state, neighbour, send, ghost,
-    updated_out,
+    kept_out, change_out, top_out,
     cells_ref, neighbour_ref, send_ref, ghost_ref,
-    vertical_out, vertical_in, lateral_out, lateral_in, change_ref,
-    value, from_plane, from_late, from_hubs, direct, result,
+    vertical_out, vertical_in, lateral_out, lateral_in,
+    value, from_plane, from_late, from_hubs, direct, result, overall,
     load_sem, table_sem, up_sem, down_sem, vin_sem, lsend_sem, lin_sem, max_send, max_recv,
 ):
     nx, ny, nz, nc = sizes
@@ -140,8 +140,10 @@
     mid = ny // 2
 
     members = [[0], list(range(1, ny))]
-    late_x, late_y, late_z = late_sets(sizes)
-    n_late = len(late_y) * late_z * 2
+    early, late_x, late_z = early_and_late(sizes)
+    n_late = ny * late_z * 2
+    early_of = [[e for e in early if e[1] in members[g]] for g in (0, 1)]
+    targets = 4 + (nz > 2)
 
     def device(px, py, pz, pc):
         return {"morton_0": px, "morton_1": py, "group_0": pz, "group_1": pc}
@@ -155,19 +157,16 @@
 
     group = jnp.minimum(y, 1)
 
-    def is_late(px, py, pz):
-        return (px >= late_x[0]) & (px <= late_x[-1]) & (py >= late_y[0]) & (py <= late_y[-1]) & (pz >= nz - late_z)
-
-    late = is_late(x, y, z)
     late_plane = (x >= late_x[0]) & (x <= late_x[-1])
-    first_device = device(0, 0, 0, HUB)
-    is_first_device = (x == 0) & (y == 0) & (z == 0) & (c == HUB)
+    late = late_plane & (z >= nz - late_z)
+    is_early = functools.reduce(jnp.logical_or, [(x == px) & (y == py) & (c == pc) for px, py, pc in early]) & (z == 0)
 
     def key(px, py, pz, pc):
         hops = jnp.minimum(px, nx - px) + jnp.minimum(py, ny - py) + jnp.minimum(pz, nz - pz)
         far = lax.div(2 * px, nx) + lax.div(2 * py, ny) + lax.div(2 * pz, nz)
         number = ((pz * ny + py) * nx + px) * 2 + pc
-        return (14 * number + 443 * hops + 620 * far - 420 * pc) * (2 * nx * ny * nz) + number
+        order = 14 * number + 443 * hops + 620 * far - 420 * pc
+        return order * (2 * nx * ny * nz) + number
 
     my_key = key(x, y, z, c)
 
@@ -175,9 +174,9 @@
         return key(p["morton_0"], p["morton_1"], p["group_0"], p["group_1"]) > my_key
 
     is_hub = ((y == 0) | (y == mid)) & (z == 0) & (c == HUB)
-    is_listener = (z == 0) & jnp.logical_not(is_hub)
-    is_teller = (z == 1) & (c != HUB)
-    is_other = (z > 1) | ((z == 1) & (c == HUB))
+    is_teller = (z == 2) & (c != HUB)
+    is_listener = (z <= 1) & jnp.logical_not(is_hub)
+    is_other = (z > 2) | ((z == 2) & (c == HUB))
     other = 1 - c
     below = device(x, y, lax.rem(z + (nz - 1) + c, nz), other)
     above = device(x, y, lax.rem(z + c, nz), other)
@@ -226,12 +225,12 @@
         for step in range(1, nx):
             greet(hub_of(lax.rem(x + step, nx), group))
 
-    @pl.when(is_first_device)
+    @pl.when(is_early)
     def _():
         def late_one(i, carry):
             px = late_x[0] + lax.rem(lax.div(i, 2), len(late_x))
             rest = lax.div(i, 2 * len(late_x))
-            greet(device(px, late_y[0] + lax.rem(rest, len(late_y)), nz - late_z + lax.div(rest, len(late_y)), lax.rem(i, 2)))
+            greet(device(px, lax.rem(rest, ny), nz - late_z + lax.div(rest, ny), lax.rem(i, 2)))
             return carry
 
         lax.fori_loop(0, len(late_x) * n_late, late_one, 0)
@@ -263,27 +262,22 @@
     def settle(ref, number, sem):
         pltpu.make_async_copy(ref.at[pl.ds(0, number)], ref.at[pl.ds(0, number)], sem).wait()
 
-    packed_z, others = z - (nz - late_z), ny - len(late_y)
-    packed_y = jnp.where(y < late_y[0], y, y - len(late_y))
-    mine = jnp.where(
-        late_plane & (packed_z >= 0),
-        ((nz - late_z) * ny + packed_z * others + packed_y) * 2 + c,
-        (z * ny + y) * 2 + c,
-    )
-
+    mine = (z * ny + y) * 2 + c
 
     @pl.when(is_hub)
     def _():
         from_plane[mine] = top
-        told = jnp.where(group == 0, len(members[0]), len(members[1])) * nx * 3
+        told = jnp.where(group == 0, len(members[0]), len(members[1])) * nx * targets
         pl.semaphore_wait(barrier, told + earlier)
         push(value.at[0], from_plane.at[mine], hub_of(x, 1 - group), 0, 0)
 
     @pl.when(late)
     def _():
-        place = ((z - (nz - late_z)) * len(late_y) + y - late_y[0]) * 2 + c
-        pl.semaphore_wait(barrier, 3 + earlier)
-        push(value.at[0], direct.at[(x - late_x[0]) * n_late + place], first_device, 0, 4)
+        place = mine - 2 * ny * (nz - late_z)
+        to_early = ((z - (nz - late_z)) * len(late_x) + x - late_x[0]) * (2 * ny) + y * 2 + c
+        pl.semaphore_wait(barrier, 2 + len(early) + earlier)
+        for px, py, pc in early:
+            push(value.at[0], direct.at[to_early], device(px, py, 0, pc), 0, 4 + (z == nz - 1).astype(jnp.int32))
         push(value.at[0], from_late.at[place], hub_of(x, 1), 0, 3)
         push(value.at[0], from_late.at[place], hub_of(x, 0), 0, 3)
 
@@ -414,7 +408,8 @@
             total[v] = total[v] + 0.5 * (
                 (flux_high[v] - flux_low[v]) - (upper * (high[v] - cells[v]) - lower * (cells[v] - low[v])))
     for v in range(VARS):
-        change_ref[v] = total[v]
+        kept_out[v] = jnp.where(live, cells[v], 0.0)
+        change_out[v] = jnp.where(live, total[v], 0.0)
 
     @pl.when(has_below)
     def _():
@@ -428,9 +423,7 @@
         copy.wait_send()
 
     def finish(highest):
-        step = COURANT / jnp.max(highest, axis=1, keepdims=True)
-        for v in range(VARS):
-            updated_out[v] = jnp.where(live, cells_ref[v] - step * change_ref[v], 0.0)
+        top_out[...] = highest
 
     def of_hubs():
         return functools.reduce(jnp.maximum, [from_hubs[i] for i in range(nx)])
@@ -438,8 +431,24 @@
     def plane_top_of(rows):
         return jnp.max(from_plane[pl.ds(0, rows)], axis=0)
 
+    def heard(number):
+        settle(from_hubs, number, max_recv.at[1])
+        overall[0] = of_hubs()
+
+        @pl.when(is_early)
+        def _():
+            last = len(late_x) * ny * 2
+            before = len(late_x) * n_late - last
+            if before:
+                settle(direct, before, max_recv.at[4])
+                overall[0] = jnp.maximum(overall[0], jnp.max(direct[pl.ds(0, before)], axis=0))
+            settle(direct, last, max_recv.at[5])
+            overall[0] = jnp.maximum(overall[0], jnp.max(direct[pl.ds(before, last)], axis=0))
+
+        return overall[0]
+
     for g in (0, 1):
-        number = len(members[g]) * nx * 3 - 1
+        number = len(members[g]) * nx * targets - 1
 
         @pl.when(is_hub & (group == g))
         def _(g=g, number=number):
@@ -452,69 +461,74 @@
             def _():
                 settle(from_plane, in_plane - n_late - 1, max_recv.at[0])
                 value[2] = plane_top_of(in_plane - n_late)
-                if g == 0:
-                    push(value.at[2], from_hubs.at[x], first_device, 2, 1)
+                for px, py, pc in early_of[g]:
+                    push(value.at[2], from_hubs.at[x], device(px, py, 0, pc), 2, 1)
+
                 settle(from_late, n_late, max_recv.at[3])
                 value[1] = jnp.maximum(value[2], jnp.max(from_late[...], axis=0))
 
             from_hubs[x] = value[1]
 
-            def tell(i, carry):
+            def tell(px, py, pz, pc):
+                push(value.at[1], from_hubs.at[x], device(px, py, pz, pc), 1, 1)
+
+            def tell_z0(i, carry):
                 py = i + members[g][0]
                 for px in range(nx):
-                    unless = (px != x) | (py != y)
-                    if g == 0 and px == 0:
-                        unless = unless & jnp.logical_not(late_plane)
-
-                    @pl.when(unless)
-                    def _(px=px):
-                        push(value.at[1], from_hubs.at[x], device(px, py, 0, HUB), 1, 1)
-
-                    push(value.at[1], from_hubs.at[x], device(px, py, 0, 1 - HUB), 1, 1)
-                    push(value.at[1], from_hubs.at[x], device(px, py, 1, 1 - HUB), 1, 1)
+                    for pc in (HUB, 1 - HUB):
+                        told = [ey for ex, ey, ec in early_of[g] if ex == px and ec == pc]
+                        unless = []
+                        if pc == HUB:
+                            unless.append((px != x) | (py != y))
+                        if told:
+                            unless.append(jnp.logical_not(late_plane) | (py != told[0]))
+                        if not unless:
+                            tell(px, py, 0, pc)
+                        else:
+                            @pl.when(functools.reduce(jnp.logical_and, unless))
+                            def _(px=px, pc=pc):
+                                tell(px, py, 0, pc)
                 return carry
 
-            lax.fori_loop(0, len(members[g]), tell, 0)
-            settle(from_hubs, nx - 1, max_recv.at[1])
-            if g == 0:
-                @pl.when(is_first_device)
-                def _():
-                    settle(direct, len(late_x) * n_late, max_recv.at[4])
-                    finish(jnp.maximum(of_hubs(), jnp.max(direct[...], axis=0)))
-
-                @pl.when(jnp.logical_not(is_first_device))
-                def _():
-                    finish(of_hubs())
-
-                @pl.when(late_plane)
-                def _():
-                    settle(from_plane, 1, max_send.at[2])
-                    settle(from_plane, number - 1, max_send.at[1])
-
-                @pl.when(jnp.logical_not(late_plane))
-                def _():
-                    settle(from_plane, number, max_send.at[1])
-            else:
-                finish(of_hubs())
+            def tell_more(i, carry):
+                py = i + members[g][0]
+                for px in range(nx):
+                    for pc in (HUB, 1 - HUB):
+                        tell(px, py, 1, pc)
+                    if nz > 2:
+                        tell(px, py, 2, 1 - HUB)
+                return carry
+
+            lax.fori_loop(0, len(members[g]), tell_z0, 0)
+            lax.fori_loop(0, len(members[g]), tell_more, 0)
+            finish(heard(nx - 1))
+
+            @pl.when(late_plane)
+            def _():
+                settle(from_plane, len(early_of[g]), max_send.at[2])
+                settle(from_plane, number - len(early_of[g]), max_send.at[1])
+
+            @pl.when(jnp.logical_not(late_plane))
+            def _():
                 settle(from_plane, number, max_send.at[1])
+
             settle(from_plane, 1, max_send.at[0])
 
     @pl.when(is_listener)
     def _():
-        settle(from_hubs, nx, max_recv.at[1])
-        finish(of_hubs())
-
-    @pl.when(is_teller)
-    def _():
-        settle(from_hubs, nx, max_recv.at[1])
-        over_all = of_hubs()
-        value[2] = over_all
-        push(value.at[2], result.at[0], device(x, y, 1, HUB), 2, 2)
-        for pz in range(2, nz):
-            for pc in (1, 0):
-                push(value.at[2], result.at[0], device(x, y, pz, pc), 2, 2)
-        finish(over_all)
-        settle(from_plane, 2 * nz - 3, max_send.at[2])
+        finish(heard(nx))
+
+    if nz > 2:
+        @pl.when(is_teller)
+        def _():
+            over_all = heard(nx)
+            value[2] = over_all
+            push(value.at[2], result.at[0], device(x, y, 2, HUB), 2, 2)
+            for pz in range(3, nz):
+                for pc in (HUB, 1 - HUB):
+                    push(value.at[2], result.at[0], device(x, y, pz, pc), 2, 2)
+            finish(over_all)
+            settle(from_plane, 2 * nz - 5, max_send.at[2])
 
     @pl.when(is_other)
     def _():
@@ -523,26 +537,38 @@
 
     @pl.when(late)
     def _():
-        settle(from_plane, 3, max_send.at[0])
+        settle(from_plane, 2 + len(early), max_send.at[0])
 
     @pl.when(jnp.logical_not(is_hub | late))
     def _():
         settle(from_plane, 2, max_send.at[0])
+
+
+def apply_kernel(kept, change, top, updated, result, sems):
+    step = COURANT / jnp.max(top[...], axis=1, keepdims=True)
+    copies = []
+    for v in range(VARS):
+        result[v] = kept[v] - step * change[v]
+        copies.append(pltpu.make_async_copy(result.at[v], updated.at[0, v], sems.at[v]))
+        copies[-1].start()
+    for copy in copies:
+        copy.wait()
 
 
 def per_device(sizes, state, patch_count, neighbour_table, send_table, ghost_table):
     nx, ny, nz, nc = sizes
-    late_x, late_y, late_z = late_sets(sizes)
-    n_late = len(late_y) * late_z * 2
+    early, late_x, late_z = early_and_late(sizes)
+    n_late = ny * late_z * 2
     any_space = pl.BlockSpec(memory_space=pl.ANY)
     vmem = pl.BlockSpec(memory_space=pltpu.VMEM)
     f32 = jnp.float32
     dma = pltpu.SemaphoreType.DMA
-    updated = pl.pallas_call(
+    block = pltpu.VMEM((VARS, SLOTS, CELLS), f32)
+    kept, change, top = pl.pallas_call(
         functools.partial(kernel, sizes),
-        out_shape=pltpu.VMEM((VARS, SLOTS, CELLS), f32),
+        out_shape=(block, block, pltpu.VMEM((1, LANES), f32)),
         in_specs=[any_space] * 4,
-        out_specs=vmem,
+        out_specs=(vmem, vmem, vmem),
         scratch_shapes=[
             pltpu.VMEM((VARS, SLOTS, CELLS), f32),
             pltpu.VMEM((4, SLOTS), jnp.int32),
@@ -552,14 +578,14 @@
             pltpu.VMEM((2, SLOTS, WIDE), f32),
             pltpu.VMEM((4, SLOTS, WIDE), f32),
             pltpu.VMEM((4, SLOTS, WIDE), f32),
-            pltpu.VMEM((VARS, SLOTS, CELLS), f32),
             pltpu.VMEM((3, 1, LANES), f32),
-            pltpu.VMEM((max(2 * ny * nz, 3 * nx * ny), 1, LANES), f32),
+            pltpu.VMEM((max(2 * ny * nz, 5 * nx * ny), 1, LANES), f32),
             pltpu.VMEM((n_late, 1, LANES), f32),
             pltpu.VMEM((nx, 1, LANES), f32),
             pltpu.VMEM((len(late_x) * n_late, 1, LANES), f32),
             pltpu.VMEM((1, 1, LANES), f32),
-            dma((VARS,)), dma((3,)), dma, dma, dma((2,)), dma((4,)), dma((4,)), dma((3,)), dma((5,)),
+            pltpu.VMEM((1, 1, LANES), f32),
+            dma((VARS,)), dma((3,)), dma, dma, dma((2,)), dma((4,)), dma((4,)), dma((3,)), dma((6,)),
         ],
         compiler_params=pltpu.CompilerParams(collective_id=0, has_side_effects=True),
         name="step",
@@ -569,7 +595,15 @@
         jnp.transpose(send_table, (2, 0, 1)),
         jnp.transpose(ghost_table, (0, 2, 1)),
     )
-    return jnp.transpose(updated[None], (0, 2, 1, 3))
+    updated = pl.pallas_call(
+        apply_kernel,
+        out_shape=jax.ShapeDtypeStruct((1, VARS, SLOTS, CELLS), f32),
+        in_specs=[vmem] * 3,
+        out_specs=any_space,
+        scratch_shapes=[block, dma((VARS,))],
+        name="apply",
+    )(*[pltpu.with_memory_space_constraint(value, pltpu.VMEM) for value in (kept, change, top)])
+    return jnp.transpose(updated, (0, 2, 1, 3))
 
 
 def solution(mesh):

time: 31.5 us -> 31.6 us (level)
  Pallas kernels: 30.7 us -> 31.4 us
  local copies, waits for them, and re-layouts: 0.64 us -> 0 us
    pallas_call x1 -> x2, Pallas kernels: 30.7 us -> 31.4 us  [the longest x1 30.6 us: per_device(): pl.pallas_call(functools.partial(kernel, sizes), out_shape=(block, block,...]
    unnamed x1 -> x0, local copies, waits for them, and re-layouts: 0.64 us -> none
where the time goes in v5:
time: 31.6 us; the launch traced here: 31.4 us
  Pallas kernels  31.4 us (99%)
    pallas_call x1, Pallas kernels, per_device(): pl.pallas_call(functools.partial(kernel, sizes), out_shape=(block, block,...  30.6 us
    pallas_call x1, Pallas kernels, per_device(): pl.pallas_call(apply_kernel, out_shape=jax.ShapeDtypeStruct((1, VARS, SLO...  0.76 us

profile of v5, /device:TPU:1, one launch (start us, length us, event | category | flops | bytes accessed | tf_op | source)
XLA Modules:
  0.0 31.4 jit_solution(3855666249337041416)
XLA Ops:
  0.0 30.6 %step.1 = (f32[5,8,512]{2,1,0:T(8,128)S(1)}, f32[5,8,512]{2,1,0:T(8,128)S(1)}, f32[1,128]{1,0:T(1,128)S(1)}) custom-call(f32[1,5,8,512]{3,2,1,0:T(8,128)} %bitcast.5, s32[1,4,8]{2,1,0:T(4,128)} %bitcast.7, s32[5,1,64]{2,1,0:T(1,128)} %bitcast.6, s32[1,4,8]{2,1,0:T(4,128)} %bitcast.8), custom_call_target="tpu_custom_call" | custom-call | tf_op jit(solution)/shard_map/step/pallas_call | solution.py:567
  30.6 0.8 %apply.1 = f32[1,5,8,512]{3,2,1,0:T(8,128)} custom-call(f32[5,8,512]{2,1,0:T(8,128)S(1)} %get-tuple-element.8.kept, f32[5,8,512]{2,1,0:T(8,128)S(1)} %get-tuple-element.9.change, f32[1,128]{1,0:T(1,128)S(1)} %get-tuple-element.10.top), custom_call_target="tpu_custom_call" | custom-call | tf_op jit(solution)/shard_map/apply/pallas_call | solution.py:598

commit v6 on v5

--- a/solution.py
+++ b/solution.py
@@ -125,10 +125,9 @@
     sizes,
     state, neighbour, send, ghost,
     kept_out, change_out, top_out,
-    cells_ref, neighbour_ref, send_ref, ghost_ref,
-    vertical_out, vertical_in, lateral_out, lateral_in,
+    cells_ref, tables_ref, send_ref, halo_out, halo_in,
     value, from_plane, from_late, from_hubs, direct, result, overall,
-    load_sem, table_sem, up_sem, down_sem, vin_sem, lsend_sem, lin_sem, max_send, max_recv,
+    load_sem, table_sem, halo_sent, halo_arrived, max_sent, max_arrived, far_up, far_down,
 ):
     nx, ny, nz, nc = sizes
     x, y, z, c = [lax.axis_index(a) for a in AXES]
@@ -181,15 +180,16 @@
     below = device(x, y, lax.rem(z + (nz - 1) + c, nz), other)
     above = device(x, y, lax.rem(z + c, nz), other)
 
-    loads = [
-        pltpu.make_async_copy(state.at[0, v], cells_ref.at[v], load_sem.at[v]) for v in range(VARS)
-    ] + [
-        pltpu.make_async_copy(neighbour.at[0], neighbour_ref, table_sem.at[0]),
+    loads = [pltpu.make_async_copy(state.at[0, v], cells_ref.at[v], load_sem) for v in range(VARS)] + [
+        pltpu.make_async_copy(neighbour.at[0], tables_ref.at[0], table_sem.at[0]),
+        pltpu.make_async_copy(ghost.at[0], tables_ref.at[1], table_sem.at[0]),
         pltpu.make_async_copy(send, send_ref, table_sem.at[1]),
-        pltpu.make_async_copy(ghost.at[0], ghost_ref, table_sem.at[2]),
     ]
     for load in loads:
         load.start()
+
+    def settle(ref, number, sem):
+        pltpu.make_async_copy(ref.at[pl.ds(0, number)], ref.at[pl.ds(0, number)], sem).wait()
 
     barrier = pltpu.get_barrier_semaphore()
 
@@ -201,8 +201,8 @@
     below_later, above_later = has_below & comes_later(below), has_above & comes_later(above)
     below_earlier = has_below & jnp.logical_not(below_later)
     above_earlier = has_above & jnp.logical_not(above_later)
-    partners = list(zip(beside + [below, above], beside_later + [below_later, above_later]))
-    earlier = sum(jnp.logical_not(f).astype(jnp.int32) for f in beside_later)
+    partners = [(beside[d], beside_later[d]) for d in (1, 2)] + [(below, below_later), (above, above_later)]
+    earlier = sum(jnp.logical_not(beside_later[d]).astype(jnp.int32) for d in (1, 2))
     earlier = earlier + below_earlier.astype(jnp.int32) + above_earlier.astype(jnp.int32)
 
     for target, later in partners:
@@ -240,10 +240,9 @@
         for px in range(nx):
             greet(hub_of(px, group))
 
-    loads[VARS].wait()
-    near = neighbour_ref[...]
-    for v in range(VARS):
-        loads[v].wait()
+    settle(tables_ref, 2, table_sem.at[0])
+    near = tables_ref[0]
+    settle(cells_ref, VARS, load_sem)
     in_row = diagonal(jnp.maximum(near[2:3, :], near[3:4, :]).astype(jnp.float32))
     live = jnp.broadcast_to(in_row, (SLOTS, CELLS)) >= 0.0
     cells = [cells_ref[v] for v in range(VARS)]
@@ -254,13 +253,10 @@
     top = jnp.max(functools.reduce(jnp.maximum, tiles_of(speed)), axis=0, keepdims=True)
     value[0] = top
 
-    def push(source, target_ref, target, phase, arrival):
+    def push(source, target_ref, target, arrival):
         pltpu.make_async_remote_copy(
-            src_ref=source, dst_ref=target_ref, send_sem=max_send.at[phase], recv_sem=max_recv.at[arrival],
+            src_ref=source, dst_ref=target_ref, send_sem=max_sent, recv_sem=max_arrived.at[arrival],
             device_id=target, device_id_type=pl.DeviceIdType.MESH).start()
-
-    def settle(ref, number, sem):
-        pltpu.make_async_copy(ref.at[pl.ds(0, number)], ref.at[pl.ds(0, number)], sem).wait()
 
     mine = (z * ny + y) * 2 + c
 
@@ -269,7 +265,7 @@
         from_plane[mine] = top
         told = jnp.where(group == 0, len(members[0]), len(members[1])) * nx * targets
         pl.semaphore_wait(barrier, told + earlier)
-        push(value.at[0], from_plane.at[mine], hub_of(x, 1 - group), 0, 0)
+        push(value.at[0], from_plane.at[mine], hub_of(x, 1 - group), 0)
 
     @pl.when(late)
     def _():
@@ -277,24 +273,27 @@
         to_early = ((z - (nz - late_z)) * len(late_x) + x - late_x[0]) * (2 * ny) + y * 2 + c
         pl.semaphore_wait(barrier, 2 + len(early) + earlier)
         for px, py, pc in early:
-            push(value.at[0], direct.at[to_early], device(px, py, 0, pc), 0, 4 + (z == nz - 1).astype(jnp.int32))
-        push(value.at[0], from_late.at[place], hub_of(x, 1), 0, 3)
-        push(value.at[0], from_late.at[place], hub_of(x, 0), 0, 3)
+            push(value.at[0], direct.at[to_early], device(px, py, 0, pc), 2 + (z == nz - 1).astype(jnp.int32))
+        push(value.at[0], from_late.at[place], hub_of(x, 1), 2)
+        push(value.at[0], from_late.at[place], hub_of(x, 0), 2)
 
     @pl.when(jnp.logical_not(is_hub | late))
     def _():
         pl.semaphore_wait(barrier, 2 + earlier)
-        push(value.at[0], from_plane.at[mine], hub_of(x, 1), 0, 0)
-        push(value.at[0], from_plane.at[mine], hub_of(x, 0), 0, 0)
-
-    vertical_out[0] = pack_face(cells, 4)
-    vertical_out[1] = pack_face(cells, 5)
-    go_down = pltpu.make_async_remote_copy(
-        src_ref=vertical_out.at[0], dst_ref=vertical_in.at[1], send_sem=down_sem, recv_sem=vin_sem.at[1],
-        device_id=below, device_id_type=pl.DeviceIdType.MESH)
-    go_up = pltpu.make_async_remote_copy(
-        src_ref=vertical_out.at[1], dst_ref=vertical_in.at[0], send_sem=up_sem, recv_sem=vin_sem.at[0],
-        device_id=above, device_id_type=pl.DeviceIdType.MESH)
+        push(value.at[0], from_plane.at[mine], hub_of(x, 1), 0)
+        push(value.at[0], from_plane.at[mine], hub_of(x, 0), 0)
+
+    def to_partner(place, partner, at_theirs):
+        return pltpu.make_async_remote_copy(
+            src_ref=halo_out.at[place], dst_ref=halo_in.at[at_theirs], send_sem=halo_sent, recv_sem=halo_arrived.at[at_theirs],
+            device_id=partner, device_id_type=pl.DeviceIdType.MESH)
+
+    def arrived(place):
+        pltpu.make_async_copy(halo_in.at[place], halo_in.at[place], halo_arrived.at[place]).wait()
+
+    halo_out[4] = pack_face(cells, 4)
+    halo_out[5] = pack_face(cells, 5)
+    go_down, go_up = to_partner(4, below, 5), to_partner(5, above, 4)
 
     @pl.when(below_earlier)
     def _():
@@ -306,15 +305,15 @@
 
     @pl.when(jnp.logical_not(has_below))
     def _():
-        vertical_in[0] = vertical_out[0]
+        halo_in[4] = halo_out[4]
 
     @pl.when(jnp.logical_not(has_above))
     def _():
-        vertical_in[1] = vertical_out[1]
+        halo_in[5] = halo_out[5]
 
     own = [pack_face(cells, face) for face in range(4)]
     own_rows = jnp.concatenate(own, axis=0)
-    loads[VARS + 1].wait()
+    loads[-1].wait()
     rows = jnp.concatenate([send_ref[t] for t in range(MSG)] + [jnp.full((SLOTS - MSG, ranks), -1, jnp.int32)], axis=0)
     columns = []
     for offset in OFFSETS:
@@ -327,54 +326,56 @@
     hot = one_hot(jnp.concatenate(columns, axis=0), 4 * SLOTS)
     messages = select_rows(hot, own_rows)
     for d in range(4):
-        lateral_out[d] = messages[d * SLOTS:(d + 1) * SLOTS]
-    lateral = [pltpu.make_async_remote_copy(
-        src_ref=lateral_out.at[d], dst_ref=lateral_in.at[3 - d], send_sem=lsend_sem.at[d], recv_sem=lin_sem.at[3 - d],
-        device_id=beside[d], device_id_type=pl.DeviceIdType.MESH) for d in range(4)]
-
-    def arrived(d):
-        return pltpu.make_async_remote_copy(
-            src_ref=lateral_out.at[d], dst_ref=lateral_in.at[d], send_sem=lsend_sem.at[d], recv_sem=lin_sem.at[d],
-            device_id=beside[d], device_id_type=pl.DeviceIdType.MESH)
-
-    for d in range(4):
+        halo_out[d] = messages[d * SLOTS:(d + 1) * SLOTS]
+    lateral = [to_partner(d, beside[d], 3 - d) for d in range(4)]
+
+    for d in (1, 2):
         @pl.when(jnp.logical_not(beside_later[d]))
         def _(d=d):
             lateral[d].start()
 
-    for d in range(4):
+    for d in (1, 2):
         @pl.when(beside_later[d])
         def _(d=d):
-            arrived(d).wait_recv()
+            arrived(d)
             lateral[d].start()
 
+    pl.semaphore_signal(far_up, inc=1, device_id=beside[1], device_id_type=pl.DeviceIdType.MESH)
+    pl.semaphore_signal(far_down, inc=1, device_id=beside[2], device_id_type=pl.DeviceIdType.MESH)
+
     @pl.when(below_later)
     def _():
-        go_up.wait_recv()
+        arrived(4)
         go_down.start()
 
     @pl.when(above_later)
     def _():
-        go_down.wait_recv()
+        arrived(5)
         go_up.start()
 
-    loads[VARS + 2].wait()
-
-    for d in range(4):
+    pl.semaphore_wait(far_up, 1)
+    lateral[3].start()
+    pl.semaphore_wait(far_down, 1)
+    lateral[0].start()
+
+
+    for d in (1, 2):
         @pl.when(jnp.logical_not(beside_later[d]))
         def _(d=d):
-            arrived(d).wait_recv()
+            arrived(d)
+
+    @pl.when(below_earlier)
+    def _():
+        arrived(4)
 
     @pl.when(above_earlier)
     def _():
-        go_down.wait_recv()
-
-    @pl.when(below_earlier)
-    def _():
-        go_up.wait_recv()
-
-    faces = jnp.concatenate([own_rows] + [lateral_in[d] for d in range(4)], axis=0)
-    far = ghost_ref[...]
+        arrived(5)
+
+    arrived(0)
+    arrived(3)
+    faces = jnp.concatenate([own_rows] + [halo_in[d] for d in range(4)], axis=0)
+    far = tables_ref[1]
     face_id = lax.broadcasted_iota(jnp.int32, (4, SLOTS), 0)
     slot_id = lane((4, SLOTS))
     local = (near >= 0) & ((near >> 3) == rank)
@@ -387,8 +388,8 @@
     hot = one_hot(jnp.concatenate(columns, axis=0), 8 * SLOTS)
     chosen = select_rows(hot, faces)
     ghosts = [chosen[k * SLOTS:(k + 1) * SLOTS] for k in range(4)]
-    ghosts.append(vertical_in[0])
-    ghosts.append(vertical_in[1])
+    ghosts.append(halo_in[4])
+    ghosts.append(halo_in[5])
 
     total = [0.0] * VARS
     at = lane((SLOTS, CELLS))
@@ -411,16 +412,13 @@
         kept_out[v] = jnp.where(live, cells[v], 0.0)
         change_out[v] = jnp.where(live, total[v], 0.0)
 
-    @pl.when(has_below)
-    def _():
-        go_down.wait_send()
-
-    @pl.when(has_above)
-    def _():
-        go_up.wait_send()
-
-    for copy in lateral:
-        copy.wait_send()
+    @pl.when(has_below & has_above)
+    def _():
+        settle(halo_out, 6, halo_sent)
+
+    @pl.when(jnp.logical_not(has_below & has_above))
+    def _():
+        settle(halo_out, 5, halo_sent)
 
     def finish(highest):
         top_out[...] = highest
@@ -432,7 +430,7 @@
         return jnp.max(from_plane[pl.ds(0, rows)], axis=0)
 
     def heard(number):
-        settle(from_hubs, number, max_recv.at[1])
+        settle(from_hubs, number, max_arrived.at[1])
         overall[0] = of_hubs()
 
         @pl.when(is_early)
@@ -440,9 +438,9 @@
             last = len(late_x) * ny * 2
             before = len(late_x) * n_late - last
             if before:
-                settle(direct, before, max_recv.at[4])
+                settle(direct, before, max_arrived.at[2])
                 overall[0] = jnp.maximum(overall[0], jnp.max(direct[pl.ds(0, before)], axis=0))
-            settle(direct, last, max_recv.at[5])
+            settle(direct, last, max_arrived.at[3])
             overall[0] = jnp.maximum(overall[0], jnp.max(direct[pl.ds(before, last)], axis=0))
 
         return overall[0]
@@ -454,23 +452,23 @@
         def _(g=g, number=number):
             @pl.when(jnp.logical_not(late_plane))
             def _():
-                settle(from_plane, in_plane - 1, max_recv.at[0])
+                settle(from_plane, in_plane - 1, max_arrived.at[0])
                 value[1] = plane_top_of(in_plane)
 
             @pl.when(late_plane)
             def _():
-                settle(from_plane, in_plane - n_late - 1, max_recv.at[0])
+                settle(from_plane, in_plane - n_late - 1, max_arrived.at[0])
                 value[2] = plane_top_of(in_plane - n_late)
                 for px, py, pc in early_of[g]:
-                    push(value.at[2], from_hubs.at[x], device(px, py, 0, pc), 2, 1)
-
-                settle(from_late, n_late, max_recv.at[3])
+                    push(value.at[2], from_hubs.at[x], device(px, py, 0, pc), 1)
+
+                settle(from_late, n_late, max_arrived.at[2])
                 value[1] = jnp.maximum(value[2], jnp.max(from_late[...], axis=0))
 
             from_hubs[x] = value[1]
 
             def tell(px, py, pz, pc):
-                push(value.at[1], from_hubs.at[x], device(px, py, pz, pc), 1, 1)
+                push(value.at[1], from_hubs.at[x], device(px, py, pz, pc), 1)
 
             def tell_z0(i, carry):
                 py = i + members[g][0]
@@ -502,17 +500,7 @@
             lax.fori_loop(0, len(members[g]), tell_z0, 0)
             lax.fori_loop(0, len(members[g]), tell_more, 0)
             finish(heard(nx - 1))
-
-            @pl.when(late_plane)
-            def _():
-                settle(from_plane, len(early_of[g]), max_send.at[2])
-                settle(from_plane, number - len(early_of[g]), max_send.at[1])
-
-            @pl.when(jnp.logical_not(late_plane))
-            def _():
-                settle(from_plane, number, max_send.at[1])
-
-            settle(from_plane, 1, max_send.at[0])
+            settle(from_plane, number + 1, max_sent)
 
     @pl.when(is_listener)
     def _():
@@ -523,36 +511,33 @@
         def _():
             over_all = heard(nx)
             value[2] = over_all
-            push(value.at[2], result.at[0], device(x, y, 2, HUB), 2, 2)
+            push(value.at[2], result.at[0], device(x, y, 2, HUB), 1)
             for pz in range(3, nz):
                 for pc in (HUB, 1 - HUB):
-                    push(value.at[2], result.at[0], device(x, y, pz, pc), 2, 2)
+                    push(value.at[2], result.at[0], device(x, y, pz, pc), 1)
             finish(over_all)
-            settle(from_plane, 2 * nz - 5, max_send.at[2])
+            settle(from_plane, 2 + 2 * nz - 5, max_sent)
 
     @pl.when(is_other)
     def _():
-        settle(result, 1, max_recv.at[2])
+        settle(result, 1, max_arrived.at[1])
         finish(result[0])
 
     @pl.when(late)
     def _():
-        settle(from_plane, 2 + len(early), max_send.at[0])
-
-    @pl.when(jnp.logical_not(is_hub | late))
-    def _():
-        settle(from_plane, 2, max_send.at[0])
-
-
-def apply_kernel(kept, change, top, updated, result, sems):
+        settle(from_plane, 2 + len(early), max_sent)
+
+    @pl.when(jnp.logical_not(is_hub | late | (is_teller & (nz > 2))))
+    def _():
+        settle(from_plane, 2, max_sent)
+
+
+def apply_kernel(kept, change, top, updated, result, sem):
     step = COURANT / jnp.max(top[...], axis=1, keepdims=True)
-    copies = []
     for v in range(VARS):
         result[v] = kept[v] - step * change[v]
-        copies.append(pltpu.make_async_copy(result.at[v], updated.at[0, v], sems.at[v]))
-        copies[-1].start()
-    for copy in copies:
-        copy.wait()
+        pltpu.make_async_copy(result.at[v], updated.at[0, v], sem).start()
+    pltpu.make_async_copy(result, updated.at[0], sem).wait()
 
 
 def per_device(sizes, state, patch_count, neighbour_table, send_table, ghost_table):
@@ -571,13 +556,10 @@
         out_specs=(vmem, vmem, vmem),
         scratch_shapes=[
             pltpu.VMEM((VARS, SLOTS, CELLS), f32),
-            pltpu.VMEM((4, SLOTS), jnp.int32),
+            pltpu.VMEM((2, 4, SLOTS), jnp.int32),
             pltpu.VMEM((MSG, 1, nx * ny), jnp.int32),
-            pltpu.VMEM((4, SLOTS), jnp.int32),
-            pltpu.VMEM((2, SLOTS, WIDE), f32),
-            pltpu.VMEM((2, SLOTS, WIDE), f32),
-            pltpu.VMEM((4, SLOTS, WIDE), f32),
-            pltpu.VMEM((4, SLOTS, WIDE), f32),
+            pltpu.VMEM((6, SLOTS, WIDE), f32),
+            pltpu.VMEM((6, SLOTS, WIDE), f32),
             pltpu.VMEM((3, 1, LANES), f32),
             pltpu.VMEM((max(2 * ny * nz, 5 * nx * ny), 1, LANES), f32),
             pltpu.VMEM((n_late, 1, LANES), f32),
@@ -585,7 +567,7 @@
             pltpu.VMEM((len(late_x) * n_late, 1, LANES), f32),
             pltpu.VMEM((1, 1, LANES), f32),
             pltpu.VMEM((1, 1, LANES), f32),
-            dma((VARS,)), dma((3,)), dma, dma, dma((2,)), dma((4,)), dma((4,)), dma((3,)), dma((6,)),
+            dma, dma((2,)), dma, dma((6,)), dma, dma((4,)), pltpu.SemaphoreType.REGULAR, pltpu.SemaphoreType.REGULAR,
         ],
         compiler_params=pltpu.CompilerParams(collective_id=0, has_side_effects=True),
         name="step",
@@ -600,7 +582,7 @@
         out_shape=jax.ShapeDtypeStruct((1, VARS, SLOTS, CELLS), f32),
         in_specs=[vmem] * 3,
         out_specs=any_space,
-        scratch_shapes=[block, dma((VARS,))],
+        scratch_shapes=[block, dma],
         name="apply",
     )(*[pltpu.with_memory_space_constraint(value, pltpu.VMEM) for value in (kept, change, top)])
     return jnp.transpose(updated, (0, 2, 1, 3))

time: 31.6 us -> 31.2 us (0.987)
  Pallas kernels: 31.4 us -> 31 us
    pallas_call x1, Pallas kernels: 30.6 us -> 30.3 us  [per_device(): pl.pallas_call(functools.partial(kernel, sizes), out_shape=(block, block,...]
where the time goes in v6:
time: 31.2 us; the launch traced here: 31 us
  Pallas kernels  31 us (99%)
    pallas_call x1, Pallas kernels, per_device(): pl.pallas_call(functools.partial(kernel, sizes), out_shape=(block, block,...  30.3 us
    pallas_call x1, Pallas kernels, per_device(): pl.pallas_call(apply_kernel, out_shape=jax.ShapeDtypeStruct((1, VARS, SLO...  0.72 us

profile of v6, /device:TPU:1, one launch (start us, length us, event | category | flops | bytes accessed | tf_op | source)
XLA Modules:
  0.0 31.0 jit_solution(4910282571525465818)
XLA Ops:
  0.0 30.3 %step.1 = (f32[5,8,512]{2,1,0:T(8,128)S(1)}, f32[5,8,512]{2,1,0:T(8,128)S(1)}, f32[1,128]{1,0:T(1,128)S(1)}) custom-call(f32[1,5,8,512]{3,2,1,0:T(8,128)} %bitcast.5, s32[1,4,8]{2,1,0:T(4,128)} %bitcast.7, s32[5,1,64]{2,1,0:T(1,128)} %bitcast.6, s32[1,4,8]{2,1,0:T(4,128)} %bitcast.8), custom_call_target="tpu_custom_call" | custom-call | tf_op jit(solution)/shard_map/step/pallas_call | solution.py:552
  30.3 0.7 %apply.1 = f32[1,5,8,512]{3,2,1,0:T(8,128)} custom-call(f32[5,8,512]{2,1,0:T(8,128)S(1)} %get-tuple-element.8.kept, f32[5,8,512]{2,1,0:T(8,128)S(1)} %get-tuple-element.9.change, f32[1,128]{1,0:T(1,128)S(1)} %get-tuple-element.10.top), custom_call_target="tpu_custom_call" | custom-call | tf_op jit(solution)/shard_map/apply/pallas_call | solution.py:580

commit v7 on v6

--- a/solution.py
+++ b/solution.py
@@ -127,7 +127,7 @@
     kept_out, change_out, top_out,
     cells_ref, tables_ref, send_ref, halo_out, halo_in,
     value, from_plane, from_late, from_hubs, direct, result, overall,
-    load_sem, table_sem, halo_sent, halo_arrived, max_sent, max_arrived, far_up, far_down,
+    load_sem, table_sem, halo_sent, halo_arrived, max_sent, max_arrived, far,
 ):
     nx, ny, nz, nc = sizes
     x, y, z, c = [lax.axis_index(a) for a in AXES]
@@ -283,17 +283,22 @@
         push(value.at[0], from_plane.at[mine], hub_of(x, 1), 0)
         push(value.at[0], from_plane.at[mine], hub_of(x, 0), 0)
 
-    def to_partner(place, partner, at_theirs):
+    def to_partner(place, partner, at_theirs, later):
+        which = 1 if later is None else later.astype(jnp.int32)
         return pltpu.make_async_remote_copy(
-            src_ref=halo_out.at[place], dst_ref=halo_in.at[at_theirs], send_sem=halo_sent, recv_sem=halo_arrived.at[at_theirs],
+            src_ref=halo_out.at[place], dst_ref=halo_in.at[at_theirs], send_sem=halo_sent, recv_sem=halo_arrived.at[which],
             device_id=partner, device_id_type=pl.DeviceIdType.MESH)
 
-    def arrived(place):
-        pltpu.make_async_copy(halo_in.at[place], halo_in.at[place], halo_arrived.at[place]).wait()
+    def arrived(number, most, which):
+        for k in range(most + 1):
+            if k:
+                @pl.when(number == k)
+                def _(k=k):
+                    settle(halo_in, k, halo_arrived.at[which])
 
     halo_out[4] = pack_face(cells, 4)
     halo_out[5] = pack_face(cells, 5)
-    go_down, go_up = to_partner(4, below, 5), to_partner(5, above, 4)
+    go_down, go_up = to_partner(4, below, 5, below_later), to_partner(5, above, 4, above_later)
 
     @pl.when(below_earlier)
     def _():
@@ -327,63 +332,47 @@
     messages = select_rows(hot, own_rows)
     for d in range(4):
         halo_out[d] = messages[d * SLOTS:(d + 1) * SLOTS]
-    lateral = [to_partner(d, beside[d], 3 - d) for d in range(4)]
+    lateral = [to_partner(d, beside[d], 3 - d, beside_later[d] if d in (1, 2) else None) for d in range(4)]
 
     for d in (1, 2):
         @pl.when(jnp.logical_not(beside_later[d]))
         def _(d=d):
             lateral[d].start()
 
+    later = sum(flag.astype(jnp.int32) for _, flag in partners)
+    arrived(later, 4, 0)
     for d in (1, 2):
         @pl.when(beside_later[d])
         def _(d=d):
-            arrived(d)
             lateral[d].start()
 
-    pl.semaphore_signal(far_up, inc=1, device_id=beside[1], device_id_type=pl.DeviceIdType.MESH)
-    pl.semaphore_signal(far_down, inc=1, device_id=beside[2], device_id_type=pl.DeviceIdType.MESH)
+    for d in (1, 2):
+        pl.semaphore_signal(far, inc=1, device_id=beside[d], device_id_type=pl.DeviceIdType.MESH)
 
     @pl.when(below_later)
     def _():
-        arrived(4)
         go_down.start()
 
     @pl.when(above_later)
     def _():
-        arrived(5)
         go_up.start()
 
-    pl.semaphore_wait(far_up, 1)
+    pl.semaphore_wait(far, 2)
     lateral[3].start()
-    pl.semaphore_wait(far_down, 1)
     lateral[0].start()
 
 
-    for d in (1, 2):
-        @pl.when(jnp.logical_not(beside_later[d]))
-        def _(d=d):
-            arrived(d)
-
-    @pl.when(below_earlier)
-    def _():
-        arrived(4)
-
-    @pl.when(above_earlier)
-    def _():
-        arrived(5)
-
-    arrived(0)
-    arrived(3)
+    arrived(earlier + 2, 6, 1)
     faces = jnp.concatenate([own_rows] + [halo_in[d] for d in range(4)], axis=0)
-    far = tables_ref[1]
+    sent_from = tables_ref[1]
     face_id = lax.broadcasted_iota(jnp.int32, (4, SLOTS), 0)
     slot_id = lane((4, SLOTS))
     local = (near >= 0) & ((near >> 3) == rank)
     place = jnp.where(local, (face_id ^ 1) * SLOTS + (near & 7), face_id * SLOTS + slot_id)
-    relative = far - rank * MSG + 2 * MSG
+    relative = sent_from - rank * MSG + 2 * MSG
     block = sum((relative >= MSG * k).astype(jnp.int32) for k in range(1, 5))
     remote = 4 * SLOTS + SLOTS * (block - (block > 2).astype(jnp.int32)) + relative - MSG * block
-    place = jnp.where(far >= 0, jnp.where(block == 2, -1, remote), place).astype(jnp.float32)
+    place = jnp.where(sent_from >= 0, jnp.where(block == 2, -1, remote), place).astype(jnp.float32)
     columns = [diagonal(place[k:k + 1, :]) for k in range(4)]
     hot = one_hot(jnp.concatenate(columns, axis=0), 8 * SLOTS)
     chosen = select_rows(hot, faces)
@@ -567,7 +556,7 @@
             pltpu.VMEM((len(late_x) * n_late, 1, LANES), f32),
             pltpu.VMEM((1, 1, LANES), f32),
             pltpu.VMEM((1, 1, LANES), f32),
-            dma, dma((2,)), dma, dma((6,)), dma, dma((4,)), pltpu.SemaphoreType.REGULAR, pltpu.SemaphoreType.REGULAR,
+            dma, dma((2,)), dma, dma((2,)), dma, dma((4,)), pltpu.SemaphoreType.REGULAR,
         ],
         compiler_params=pltpu.CompilerParams(collective_id=0, has_side_effects=True),
         name="step",

time: 31.2 us -> 31.1 us (level)
  no operation moved by 1% of the time
where the time goes in v7:
time: 31.1 us; the launch traced here: 31 us
  Pallas kernels  30.9 us (99%)
    pallas_call x1, Pallas kernels, per_device(): pl.pallas_call(functools.partial(kernel, sizes), out_shape=(block, block,...  30.2 us
    pallas_call x1, Pallas kernels, per_device(): pl.pallas_call(apply_kernel, out_shape=jax.ShapeDtypeStruct((1, VARS, SLO...  0.72 us

profile of v7, /device:TPU:1, one launch (start us, length us, event | category | flops | bytes accessed | tf_op | source)
XLA Modules:
  0.0 31.0 jit_solution(8587967575752357245)
XLA Ops:
  0.0 30.2 %step.1 = (f32[5,8,512]{2,1,0:T(8,128)S(1)}, f32[5,8,512]{2,1,0:T(8,128)S(1)}, f32[1,128]{1,0:T(1,128)S(1)}) custom-call(f32[1,5,8,512]{3,2,1,0:T(8,128)} %bitcast.5, s32[1,4,8]{2,1,0:T(4,128)} %bitcast.7, s32[5,1,64]{2,1,0:T(1,128)} %bitcast.6, s32[1,4,8]{2,1,0:T(4,128)} %bitcast.8), custom_call_target="tpu_custom_call" | custom-call | tf_op jit(solution)/shard_map/step/pallas_call | solution.py:541
  30.2 0.7 %apply.1 = f32[1,5,8,512]{3,2,1,0:T(8,128)} custom-call(f32[5,8,512]{2,1,0:T(8,128)S(1)} %get-tuple-element.8.kept, f32[5,8,512]{2,1,0:T(8,128)S(1)} %get-tuple-element.9.change, f32[1,128]{1,0:T(1,128)S(1)} %get-tuple-element.10.top), custom_call_target="tpu_custom_call" | custom-call | tf_op jit(solution)/shard_map/apply/pallas_call | solution.py:569

commit v8 on v7

--- a/solution.py
+++ b/solution.py
@@ -129,6 +129,14 @@
     value, from_plane, from_late, from_hubs, direct, result, overall,
     load_sem, table_sem, halo_sent, halo_arrived, max_sent, max_arrived, far,
 ):
+    loads = [pltpu.make_async_copy(state.at[0, v], cells_ref.at[v], load_sem) for v in range(VARS)] + [
+        pltpu.make_async_copy(neighbour.at[0], tables_ref.at[0], table_sem.at[0]),
+        pltpu.make_async_copy(ghost.at[0], tables_ref.at[1], table_sem.at[0]),
+        pltpu.make_async_copy(send, send_ref, table_sem.at[1]),
+    ]
+    for load in loads:
+        load.start()
+
     nx, ny, nz, nc = sizes
     x, y, z, c = [lax.axis_index(a) for a in AXES]
     rank = x * ny + y
@@ -155,6 +163,27 @@
         return device(lax.div(j, ny), lax.rem(j, ny), z, c)
 
     group = jnp.minimum(y, 1)
+    is_hub = ((y == 0) | (y == mid)) & (z == 0) & (c == HUB)
+
+    barrier = pltpu.get_barrier_semaphore()
+
+    def greet(target):
+        pl.semaphore_signal(barrier, inc=1, device_id=target, device_id_type=pl.DeviceIdType.MESH)
+
+    @pl.when(is_hub)
+    def _():
+        def plane(i, carry):
+            py, pz, pc = lax.rem(lax.div(i, 2), ny), lax.div(i, 2 * ny), lax.rem(i, 2)
+
+            @pl.when((py != y) | (pz != 0) | (pc != HUB))
+            def _():
+                greet(device(x, py, pz, pc))
+
+            return carry
+
+        lax.fori_loop(0, in_plane, plane, 0)
+        for step in range(1, nx):
+            greet(hub_of(lax.rem(x + step, nx), group))
 
     late_plane = (x >= late_x[0]) & (x <= late_x[-1])
     late = late_plane & (z >= nz - late_z)
@@ -172,7 +201,6 @@
     def comes_later(p):
         return key(p["morton_0"], p["morton_1"], p["group_0"], p["group_1"]) > my_key
 
-    is_hub = ((y == 0) | (y == mid)) & (z == 0) & (c == HUB)
     is_teller = (z == 2) & (c != HUB)
     is_listener = (z <= 1) & jnp.logical_not(is_hub)
     is_other = (z > 2) | ((z == 2) & (c == HUB))
@@ -180,21 +208,8 @@
     below = device(x, y, lax.rem(z + (nz - 1) + c, nz), other)
     above = device(x, y, lax.rem(z + c, nz), other)
 
-    loads = [pltpu.make_async_copy(state.at[0, v], cells_ref.at[v], load_sem) for v in range(VARS)] + [
-        pltpu.make_async_copy(neighbour.at[0], tables_ref.at[0], table_sem.at[0]),
-        pltpu.make_async_copy(ghost.at[0], tables_ref.at[1], table_sem.at[0]),
-        pltpu.make_async_copy(send, send_ref, table_sem.at[1]),
-    ]
-    for load in loads:
-        load.start()
-
     def settle(ref, number, sem):
         pltpu.make_async_copy(ref.at[pl.ds(0, number)], ref.at[pl.ds(0, number)], sem).wait()
-
-    barrier = pltpu.get_barrier_semaphore()
-
-    def greet(target):
-        pl.semaphore_signal(barrier, inc=1, device_id=target, device_id_type=pl.DeviceIdType.MESH)
 
     beside = [at_rank(o) for o in OFFSETS]
     beside_later = [comes_later(p) for p in beside]
@@ -209,21 +224,6 @@
         @pl.when(later)
         def _(target=target):
             greet(target)
-
-    @pl.when(is_hub)
-    def _():
-        def plane(i, carry):
-            py, pz, pc = lax.rem(lax.div(i, 2), ny), lax.div(i, 2 * ny), lax.rem(i, 2)
-
-            @pl.when((py != y) | (pz != 0) | (pc != HUB))
-            def _():
-                greet(device(x, py, pz, pc))
-
-            return carry
-
-        lax.fori_loop(0, in_plane, plane, 0)
-        for step in range(1, nx):
-            greet(hub_of(lax.rem(x + step, nx), group))
 
     @pl.when(is_early)
     def _():
@@ -260,13 +260,6 @@
 
     mine = (z * ny + y) * 2 + c
 
-    @pl.when(is_hub)
-    def _():
-        from_plane[mine] = top
-        told = jnp.where(group == 0, len(members[0]), len(members[1])) * nx * targets
-        pl.semaphore_wait(barrier, told + earlier)
-        push(value.at[0], from_plane.at[mine], hub_of(x, 1 - group), 0)
-
     @pl.when(late)
     def _():
         place = mine - 2 * ny * (nz - late_z)
@@ -276,6 +269,13 @@
             push(value.at[0], direct.at[to_early], device(px, py, 0, pc), 2 + (z == nz - 1).astype(jnp.int32))
         push(value.at[0], from_late.at[place], hub_of(x, 1), 2)
         push(value.at[0], from_late.at[place], hub_of(x, 0), 2)
+
+    @pl.when(is_hub)
+    def _():
+        from_plane[mine] = top
+        told = jnp.where(group == 0, len(members[0]), len(members[1])) * nx * targets
+        pl.semaphore_wait(barrier, told + earlier)
+        push(value.at[0], from_plane.at[mine], hub_of(x, 1 - group), 0)
 
     @pl.when(jnp.logical_not(is_hub | late))
     def _():

time: 31.1 us -> 31.1 us (level)
  no operation moved by 1% of the time
where the time goes in v8:
time: 31.1 us; the launch traced here: 30.9 us
  Pallas kernels  30.9 us (99%)
    pallas_call x1, Pallas kernels, per_device(): pl.pallas_call(functools.partial(kernel, sizes), out_shape=(block, block,...  30.2 us
    pallas_call x1, Pallas kernels, per_device(): pl.pallas_call(apply_kernel, out_shape=jax.ShapeDtypeStruct((1, VARS, SLO...  0.72 us

profile of v8, /device:TPU:1, one launch (start us, length us, event | category | flops | bytes accessed | tf_op | source)
XLA Modules:
  0.0 30.9 jit_solution(27396301519350338)
XLA Ops:
  0.0 30.2 %step.1 = (f32[5,8,512]{2,1,0:T(8,128)S(1)}, f32[5,8,512]{2,1,0:T(8,128)S(1)}, f32[1,128]{1,0:T(1,128)S(1)}) custom-call(f32[1,5,8,512]{3,2,1,0:T(8,128)} %bitcast.5, s32[1,4,8]{2,1,0:T(4,128)} %bitcast.7, s32[5,1,64]{2,1,0:T(1,128)} %bitcast.6, s32[1,4,8]{2,1,0:T(4,128)} %bitcast.8), custom_call_target="tpu_custom_call" | custom-call | tf_op jit(solution)/shard_map/step/pallas_call | solution.py:541
  30.2 0.7 %apply.1 = f32[1,5,8,512]{3,2,1,0:T(8,128)} custom-call(f32[5,8,512]{2,1,0:T(8,128)S(1)} %get-tuple-element.8.kept, f32[5,8,512]{2,1,0:T(8,128)S(1)} %get-tuple-element.9.change, f32[1,128]{1,0:T(1,128)S(1)} %get-tuple-element.10.top), custom_call_target="tpu_custom_call" | custom-call | tf_op jit(solution)/shard_map/apply/pallas_call | solution.py:569

commit v9 on v8

--- a/solution.py
+++ b/solution.py
@@ -129,9 +129,10 @@
     value, from_plane, from_late, from_hubs, direct, result, overall,
     load_sem, table_sem, halo_sent, halo_arrived, max_sent, max_arrived, far,
 ):
-    loads = [pltpu.make_async_copy(state.at[0, v], cells_ref.at[v], load_sem) for v in range(VARS)] + [
+    loads = [
         pltpu.make_async_copy(neighbour.at[0], tables_ref.at[0], table_sem.at[0]),
         pltpu.make_async_copy(ghost.at[0], tables_ref.at[1], table_sem.at[0]),
+    ] + [pltpu.make_async_copy(state.at[0, v], cells_ref.at[v], load_sem) for v in range(VARS)] + [
         pltpu.make_async_copy(send, send_ref, table_sem.at[1]),
     ]
     for load in loads:
@@ -242,9 +243,9 @@
 
     settle(tables_ref, 2, table_sem.at[0])
     near = tables_ref[0]
-    settle(cells_ref, VARS, load_sem)
     in_row = diagonal(jnp.maximum(near[2:3, :], near[3:4, :]).astype(jnp.float32))
     live = jnp.broadcast_to(in_row, (SLOTS, CELLS)) >= 0.0
+    settle(cells_ref, VARS, load_sem)
     cells = [cells_ref[v] for v in range(VARS)]
     prims = primitives(cells)
     velocity, pressure, sound = prims

time: 31.1 us -> 31.1 us (level)
  no operation moved by 1% of the time
where the time goes in v9:
time: 31.1 us; the launch traced here: 30.9 us
  Pallas kernels  30.9 us (99%)
    pallas_call x1, Pallas kernels, per_device(): pl.pallas_call(functools.partial(kernel, sizes), out_shape=(block, block,...  30.2 us
    pallas_call x1, Pallas kernels, per_device(): pl.pallas_call(apply_kernel, out_shape=jax.ShapeDtypeStruct((1, VARS, SLO...  0.72 us

profile of v9, /device:TPU:1, one launch (start us, length us, event | category | flops | bytes accessed | tf_op | source)
XLA Modules:
  0.0 30.9 jit_solution(15353856347803962091)
XLA Ops:
  0.0 30.2 %step.1 = (f32[5,8,512]{2,1,0:T(8,128)S(1)}, f32[5,8,512]{2,1,0:T(8,128)S(1)}, f32[1,128]{1,0:T(1,128)S(1)}) custom-call(f32[1,5,8,512]{3,2,1,0:T(8,128)} %bitcast.5, s32[1,4,8]{2,1,0:T(4,128)} %bitcast.7, s32[5,1,64]{2,1,0:T(1,128)} %bitcast.6, s32[1,4,8]{2,1,0:T(4,128)} %bitcast.8), custom_call_target="tpu_custom_call" | custom-call | tf_op jit(solution)/shard_map/step/pallas_call | solution.py:542
  30.2 0.7 %apply.1 = f32[1,5,8,512]{3,2,1,0:T(8,128)} custom-call(f32[5,8,512]{2,1,0:T(8,128)S(1)} %get-tuple-element.8.kept, f32[5,8,512]{2,1,0:T(8,128)S(1)} %get-tuple-element.9.change, f32[1,128]{1,0:T(1,128)S(1)} %get-tuple-element.10.top), custom_call_target="tpu_custom_call" | custom-call | tf_op jit(solution)/shard_map/apply/pallas_call | solution.py:570

commit v10 on v9

--- a/solution.py
+++ b/solution.py
@@ -264,10 +264,11 @@
     @pl.when(late)
     def _():
         place = mine - 2 * ny * (nz - late_z)
-        to_early = ((z - (nz - late_z)) * len(late_x) + x - late_x[0]) * (2 * ny) + y * 2 + c
+        turned = lax.rem(x + (len(late_x) - nx // 2 - 1), len(late_x))
+        to_early = ((z - (nz - late_z)) * len(late_x) + turned) * (2 * ny) + y * 2 + c
         pl.semaphore_wait(barrier, 2 + len(early) + earlier)
         for px, py, pc in early:
-            push(value.at[0], direct.at[to_early], device(px, py, 0, pc), 2 + (z == nz - 1).astype(jnp.int32))
+            push(value.at[0], direct.at[to_early], device(px, py, 0, pc), 2 + ((z == nz - 1) & (x == nx // 2)).astype(jnp.int32))
         push(value.at[0], from_late.at[place], hub_of(x, 1), 2)
         push(value.at[0], from_late.at[place], hub_of(x, 0), 2)
 
@@ -425,7 +426,7 @@
 
         @pl.when(is_early)
         def _():
-            last = len(late_x) * ny * 2
+            last = ny * 2
             before = len(late_x) * n_late - last
             if before:
                 settle(direct, before, max_arrived.at[2])

time: 31.1 us -> 31.1 us (level)
  no operation moved by 1% of the time
where the time goes in v10:
time: 31.1 us; the launch traced here: 30.9 us
  Pallas kernels  30.9 us (99%)
    pallas_call x1, Pallas kernels, per_device(): pl.pallas_call(functools.partial(kernel, sizes), out_shape=(block, block,...  30.2 us
    pallas_call x1, Pallas kernels, per_device(): pl.pallas_call(apply_kernel, out_shape=jax.ShapeDtypeStruct((1, VARS, SLO...  0.72 us

profile of v10, /device:TPU:1, one launch (start us, length us, event | category | flops | bytes accessed | tf_op | source)
XLA Modules:
  0.0 30.9 jit_solution(4890541853083901683)
XLA Ops:
  0.0 30.2 %step.1 = (f32[5,8,512]{2,1,0:T(8,128)S(1)}, f32[5,8,512]{2,1,0:T(8,128)S(1)}, f32[1,128]{1,0:T(1,128)S(1)}) custom-call(f32[1,5,8,512]{3,2,1,0:T(8,128)} %bitcast.5, s32[1,4,8]{2,1,0:T(4,128)} %bitcast.7, s32[5,1,64]{2,1,0:T(1,128)} %bitcast.6, s32[1,4,8]{2,1,0:T(4,128)} %bitcast.8), custom_call_target="tpu_custom_call" | custom-call | tf_op jit(solution)/shard_map/step/pallas_call | solution.py:543
  30.2 0.7 %apply.1 = f32[1,5,8,512]{3,2,1,0:T(8,128)} custom-call(f32[5,8,512]{2,1,0:T(8,128)S(1)} %get-tuple-element.8.kept, f32[5,8,512]{2,1,0:T(8,128)S(1)} %get-tuple-element.9.change, f32[1,128]{1,0:T(1,128)S(1)} %get-tuple-element.10.top), custom_call_target="tpu_custom_call" | custom-call | tf_op jit(solution)/shard_map/apply/pallas_call | solution.py:571
